TPU v7x, 8 devices: a whole 2x2x1 slice. The times are simulated.
8 devices in a mesh: dp: 2 (over z, y), sp: 4 (over x, core).
Axes of the slice: x: 2, y: 2, z: 1, core: 2. Of those that a mesh axis runs over, the one named last changes fastest.
Arguments:
- hidden: bfloat16 [512, 6144], P(('dp', 'sp')), parts along dimension 0
- w_q: bfloat16 [6144, 6144], replicated
- w_k: bfloat16 [6144, 1024], replicated
- w_v: bfloat16 [6144, 1024], replicated
- w_o: bfloat16 [6144, 6144], replicated
- expert_ids: int32 [512, 2], P(('dp', 'sp')), parts along dimension 0
- router_probs: float32 [512, 8], P(('dp', 'sp')), parts along dimension 0
Outputs:
- output 1: bfloat16 [512, 6144], P(('dp', 'sp')), parts along dimension 0
- output 2: bfloat16 [16, 256, 6144], P(('dp', 'sp')), parts along dimension 0
There are 2 independent parts. A program takes and returns all parts, laid end to end along the dimension named above; an argument that names none is the same for every part.
All inputs are finite; a program needn't handle non-finite values.
Results may differ from a plain program's by a relative error of at most 0.00851991.
Values are sent between devices in bfloat16 or wider.
A program may use at most 1 GiB of HBM per device.

v0:
```python
import math
import jax
import jax.numpy as jnp
from jax import lax
from jax.sharding import PartitionSpec as P

HEAD_DIM = 128
SCORE_SCALE = 1.0 / math.sqrt(HEAD_DIM)


def route_rows(hidden_out, expert_ids, router_probs):
    tok_dev, width = hidden_out.shape
    experts = router_probs.shape[1]
    picked = jnp.take_along_axis(router_probs, expert_ids, axis=1)
    gate_w = picked / jnp.sum(picked, axis=1, keepdims=True)
    gated = (gate_w[:, :, None] * hidden_out[:, None, :].astype(jnp.float32)).astype(jnp.bfloat16)
    token_hits = jnp.sum((expert_ids[:, :, None] == jnp.arange(experts)).astype(jnp.int32), axis=1)
    earlier = jnp.cumsum(token_hits, axis=0) - token_hits
    slot_rank = jnp.take_along_axis(earlier, expert_ids, axis=1)
    send_buf = jnp.zeros((experts, tok_dev, width), jnp.bfloat16)
    return send_buf.at[expert_ids, slot_rank].set(gated, unique_indices=True)


def solution(mesh):
    group = mesh.shape['sp']
    row_spec = P(('dp', 'sp'), None)
    buf_spec = P(('dp', 'sp'), None, None)

    def device_step(x_loc, w_q, w_k, w_v, w_o, ids_loc, probs_loc):
        tok_dev = x_loc.shape[0]
        seq_len = tok_dev * group
        n_heads = w_q.shape[1] // HEAD_DIM
        kv_heads = w_k.shape[1] // HEAD_DIM
        kv_copies = max(1, group // kv_heads)
        head_dev = n_heads // group
        kv_dev = kv_heads * kv_copies // group
        q_loc = jnp.dot(x_loc, w_q, preferred_element_type=jnp.float32).astype(jnp.bfloat16).reshape(tok_dev, n_heads, HEAD_DIM)
        k_loc = jnp.dot(x_loc, w_k, preferred_element_type=jnp.float32).astype(jnp.bfloat16).reshape(tok_dev, kv_heads, HEAD_DIM)
        v_loc = jnp.dot(x_loc, w_v, preferred_element_type=jnp.float32).astype(jnp.bfloat16).reshape(tok_dev, kv_heads, HEAD_DIM)
        k_loc = jnp.repeat(k_loc, kv_copies, axis=1)
        v_loc = jnp.repeat(v_loc, kv_copies, axis=1)
        q_seq = lax.all_to_all(q_loc, 'sp', 1, 0, tiled=True)
        k_seq = lax.all_to_all(k_loc, 'sp', 1, 0, tiled=True)
        v_seq = lax.all_to_all(v_loc, 'sp', 1, 0, tiled=True)
        q_grp = q_seq.reshape(seq_len, kv_dev, head_dev // kv_dev, HEAD_DIM)
        scores = jnp.einsum('qgmd,kgd->gmqk', q_grp, k_seq, preferred_element_type=jnp.float32) * SCORE_SCALE
        positions = jnp.arange(seq_len)
        causal = positions[:, None] >= positions[None, :]
        weights = jax.nn.softmax(jnp.where(causal, scores, -1e30), axis=-1).astype(jnp.bfloat16)
        attn_seq = jnp.einsum('gmqk,kgd->qgmd', weights, v_seq, preferred_element_type=jnp.float32).astype(jnp.bfloat16)
        attn_seq = attn_seq.reshape(seq_len, head_dev, HEAD_DIM)
        attn_loc = lax.all_to_all(attn_seq, 'sp', 0, 1, tiled=True).reshape(tok_dev, n_heads * HEAD_DIM)
        out_proj = jnp.dot(attn_loc, w_o, preferred_element_type=jnp.float32)
        hidden_out = (x_loc.astype(jnp.float32) + out_proj).astype(jnp.bfloat16)
        send_buf = route_rows(hidden_out, ids_loc, probs_loc)
        recv_buf = lax.all_to_all(send_buf, 'sp', 0, 1, tiled=True)
        return hidden_out, recv_buf

    return jax.shard_map(device_step, mesh=mesh, in_specs=(row_spec, P(), P(), P(), P(), row_spec, row_spec), out_specs=(row_spec, buf_spec), check_vma=False)
```

profile of v0, /device:TPU:0, one launch (start us, length us, event | category | flops | bytes accessed | tf_op | source)
XLA Modules:
  0.0 250.3 jit_solution(9296806549784632654)
XLA Ops:
  0.7 7.2 %fusion.10 = bf16[8,8,8,128]{3,2,1,0:T(8,128)(2,1)S(1)} fusion(bf16[64,6144]{1,0:T(8,128)(2,1)} %param.7, bf16[6144,1024]{1,0:T(8,128)(2,1)} %param.9), kind=kOutput, calls=%fused_computation.21 | convolution fusion | flops 805371904 | bytes 13500416 | tf_op jit(solution)/shard_map/dot_general | solution.py:38
  7.8 0.7 copy.137
  8.5 4.6 %all-to-all-start.1 = ((bf16[64,8,128]{2,0,1:T(8,128)(2,1)}), bf16[64,8,128]{2,0,1:T(8,128)(2,1)S(1)}, u32[]{:S(2)}, u32[]{:S(2)}) async-start(bf16[64,8,128]{2,0,1:T(8,128)(2,1)} %bitcast.78), calls=%async_computation.1 | async-start | bytes 262144 | tf_op jit(solution)/shard_map/all_to_all | solution.py:43
  13.1 6.9 %fusion.9 = bf16[8,8,8,128]{3,2,1,0:T(8,128)(2,1)S(1)} fusion(bf16[64,6144]{1,0:T(8,128)(2,1)S(1)} %copy-done.1, bf16[6144,1024]{1,0:T(8,128)(2,1)} %param.10), kind=kOutput, calls=%fused_computation.20 | convolution fusion | flops 805371904 | bytes 13500416 | tf_op jit(solution)/shard_map/dot_general | solution.py:39
  20.0 0.7 copy.138
  20.7 3.3 %all-to-all-start = ((bf16[64,8,128]{2,0,1:T(8,128)(2,1)}), bf16[64,8,128]{2,0,1:T(8,128)(2,1)S(1)}, u32[]{:S(2)}, u32[]{:S(2)}) async-start(bf16[64,8,128]{2,0,1:T(8,128)(2,1)} %bitcast.79), calls=%async_computation | async-start | bytes 262144 | tf_op jit(solution)/shard_map/all_to_all | solution.py:44
  24.1 27.3 %fusion.8 = bf16[8,48,8,128]{3,2,1,0:T(8,128)(2,1)S(1)} fusion(bf16[64,6144]{1,0:T(8,128)(2,1)S(1)} %copy-done.1, bf16[6144,6144]{1,0:T(8,128)(2,1)} %param.8), kind=kOutput, calls=%fused_computation.17 | convolution fusion | flops 4832231424 | bytes 77070336 | tf_op jit(solution)/shard_map/dot_general | solution.py:37
  51.4 1.1 copy.136
  52.5 3.5 %all-to-all-start.2 = ((bf16[64,48,128]{2,0,1:T(8,128)(2,1)}), bf16[64,48,128]{2,0,1:T(8,128)(2,1)S(1)}, u32[]{:S(2)}, u32[]{:S(2)}) async-start(bf16[64,48,128]{2,0,1:T(8,128)(2,1)} %bitcast.77), calls=%async_computation.2 | async-start | bytes 1572864 | tf_op jit(solution)/shard_map/all_to_all | solution.py:42
  56.1 11.3 %all-to-all-done.2 = bf16[64,48,128]{2,0,1:T(8,128)(2,1)S(1)} async-done(((bf16[64,48,128]{2,0,1:T(8,128)(2,1)}), bf16[64,48,128]{2,0,1:T(8,128)(2,1)S(1)}, u32[]{:S(2)}, u32[]{:S(2)}) %all-to-all-start.2) | async-done | bytes 786464 | tf_op jit(solution)/shard_map/all_to_all | solution.py:42
  67.4 2.8 %fusion.19 = (f32[2,6,256]{2,1,0:T(8,128)S(1)}, f32[2,6,256,256]{2,3,1,0:T(8,128)}) fusion(pred[256,256]{0,1:T(8,128)(4,1)S(1)} %iota_compare_fusion, bf16[256,2,128,1]{2,0,3,1:T(8,128)(2,1)S(1)} %bitcast.90, bf16[256,2,6,128]{3,0,2,1:T(8,128)(2,1)S(1)} %bitcast.86), kind=kOutput, calls=%fused_computation.44 | convolution fusion | flops 204472576 | bytes 4141056 | tf_op jit(solution)/shard_map/sub | solution.py:49
  70.2 2.3 fusion.7
  72.6 1.7 copy.113
  74.3 3.7 %all-to-all-start.3 = ((bf16[256,12,128]{2,1,0:T(8,128)(2,1)}), bf16[256,12,128]{2,1,0:T(8,128)(2,1)S(1)}, u32[]{:S(2)}, u32[]{:S(2)}) async-start(bf16[256,12,128]{2,1,0:T(8,128)(2,1)} %copy.113), calls=%async_computation.3 | async-start | bytes 2097152 | tf_op jit(solution)/shard_map/all_to_all | solution.py:52
  78.4 1.0 gather_fusion.1
  79.8 1.3 gather_fusion
  81.6 10.4 %all-to-all-done.3 = bf16[256,12,128]{2,1,0:T(8,128)(2,1)S(1)} async-done(((bf16[256,12,128]{2,1,0:T(8,128)(2,1)}), bf16[256,12,128]{2,1,0:T(8,128)(2,1)S(1)}, u32[]{:S(2)}, u32[]{:S(2)}) %all-to-all-start.3) | async-done | bytes 786464 | tf_op jit(solution)/shard_map/all_to_all | solution.py:52
  92.9 28.8 %fusion.20 = (f32[64,6144]{1,0:T(8,128)}, bf16[64,6144]{1,0:T(8,128)(2,1)}) fusion(bf16[64,6144]{1,0:T(8,128)(2,1)S(1)} %reshape.51, bf16[6144,6144]{1,0:T(8,128)(2,1)} %param.11, bf16[64,6144]{1,0:T(8,128)(2,1)S(1)} %copy-done.1), kind=kOutput, calls=%fused_computation.45 | convolution fusion | flops 4833411072 | bytes 79429632 | tf_op jit(solution)/shard_map/dot_general | solution.py:53
  121.7 2.6 %multiply_convert_fusion = bf16[64,2,6144]{2,1,0:T(2,128)(2,1)S(1)} fusion(f32[64,6144]{1,0:T(8,128)} %get-tuple-element.4, f32[64,2]{1,0:T(8,128)S(1)} %copy.122), kind=kLoop, calls=%fused_computation.8 | loop fusion | flops 1572864 | bytes 3146240 | tf_op jit(solution)/shard_map/convert_element_type | solution.py:16
  124.3 0.6 reshape.66
  125.0 3.5 %broadcast_in_dim.34 = bf16[8,64,6144]{2,1,0:T(8,128)(2,1)} broadcast(bf16[]{:T(256)} %constant.25.clone.1), dimensions={} | broadcast | bytes 6291458 | tf_op jit(solution)/shard_map/broadcast_in_dim | solution.py:20
  128.4 44.4 %scatter_fusion = bf16[8,64,6144]{2,1,0:T(8,128)(2,1)} fusion(bf16[8,64,6144]{2,1,0:T(8,128)(2,1)} %broadcast_in_dim.34, s32[128]{0:T(128)S(1)} %reshape.64, bf16[128,6144]{1,0:T(8,128)(2,1)S(1)} %reshape.66), kind=kCustom, calls=%fused_computation.2 | custom fusion | bytes 4719616 | tf_op jit(solution)/shard_map/scatter | solution.py:21
  172.8 74.3 %all_to_all.84 = bf16[8,64,6144]{2,1,0:T(8,128)(2,1)S(1)} all-to-all(bf16[8,64,6144]{2,1,0:T(8,128)(2,1)} %scatter_fusion), channel_id=1, replica_groups=mesh['dp'=2,'sp'=4] {'sp'}, dimensions={0} | all-to-all | bytes 12582912 | tf_op jit(solution)/shard_map/all_to_all | solution.py:56
  247.1 3.1 %copy.123 = bf16[2,4,64,6144]{3,2,1,0:T(8,128)(2,1)} copy(bf16[2,4,64,6144]{3,2,0,1:T(8,128)(2,1)S(1)} %bitcast.81) | data formatting | bytes 12582912 | tf_op jit(solution)/shard_map/all_to_all | solution.py:56
  (31 shorter events, 2.2 us)
Async XLA Ops:
  0.6 77.7 %copy-start = (f32[64,8]{0,1:T(8,128)S(1)}, f32[64,8]{0,1:T(8,128)}, u32[]{:S(2)}) copy-start(f32[64,8]{0,1:T(8,128)} %param.13) | copy-start | bytes 6148
  0.6 12.5 %copy-start.1 = (bf16[64,6144]{1,0:T(8,128)(2,1)S(1)}, bf16[64,6144]{1,0:T(8,128)(2,1)}, u32[]{:S(2)}) copy-start(bf16[64,6144]{1,0:T(8,128)(2,1)} %param.7) | copy-start | bytes 2359300
  8.5 12.2 %all-to-all-start.1 = ((bf16[64,8,128]{2,0,1:T(8,128)(2,1)}), bf16[64,8,128]{2,0,1:T(8,128)(2,1)S(1)}, u32[]{:S(2)}, u32[]{:S(2)}) async-start(bf16[64,8,128]{2,0,1:T(8,128)(2,1)} %bitcast.78), calls=%async_computation.1 | async-start | bytes 262144 | tf_op jit(solution)/shard_map/all_to_all | solution.py:43
  20.7 31.8 %all-to-all-start = ((bf16[64,8,128]{2,0,1:T(8,128)(2,1)}), bf16[64,8,128]{2,0,1:T(8,128)(2,1)S(1)}, u32[]{:S(2)}, u32[]{:S(2)}) async-start(bf16[64,8,128]{2,0,1:T(8,128)(2,1)} %bitcast.79), calls=%async_computation | async-start | bytes 262144 | tf_op jit(solution)/shard_map/all_to_all | solution.py:44
  51.4 4.7 %copy-start.2 = (s32[64,2]{0,1:T(2,128)S(1)}, s32[64,2]{0,1:T(2,128)}, u32[]{:S(2)}) copy-start(s32[64,2]{0,1:T(2,128)} %param.12) | copy-start | bytes 1540
  52.5 14.9 %all-to-all-start.2 = ((bf16[64,48,128]{2,0,1:T(8,128)(2,1)}), bf16[64,48,128]{2,0,1:T(8,128)(2,1)S(1)}, u32[]{:S(2)}, u32[]{:S(2)}) async-start(bf16[64,48,128]{2,0,1:T(8,128)(2,1)} %bitcast.77), calls=%async_computation.2 | async-start | bytes 1572864 | tf_op jit(solution)/shard_map/all_to_all | solution.py:42
  74.3 17.7 %all-to-all-start.3 = ((bf16[256,12,128]{2,1,0:T(8,128)(2,1)}), bf16[256,12,128]{2,1,0:T(8,128)(2,1)S(1)}, u32[]{:S(2)}, u32[]{:S(2)}) async-start(bf16[256,12,128]{2,1,0:T(8,128)(2,1)} %copy.113), calls=%async_computation.3 | async-start | bytes 2097152 | tf_op jit(solution)/shard_map/all_to_all | solution.py:52
where the time goes:
time: 251 us; the launch traced here: 250 us
  matrix products  75.3 us (30%)
  blocking collectives  74.3 us (30%)
  local copies, waits for them, and re-layouts  60 us (24%)
  waiting for transfers between devices  21.7 us (9%)
  starting transfers between devices  15.1 us (6%)
  other arithmetic  2.83 us (1%)
    all_to_all x1, blocking collectives, device_step(): recv_buf = lax.all_to_all(send_buf, 'sp', 0, 1, tiled=True)  74.3 us
    scatter x1, local copies, waits for them, and re-layouts, route_rows(): return send_buf.at[expert_ids, slot_rank].set(gated, unique_indices=True)  44.4 us
    dot_general x1, matrix products, device_step(): out_proj = jnp.dot(attn_loc, w_o, preferred_element_type=jnp.float32)  28.8 us
    dot_general x1, matrix products, device_step(): jnp.dot(x_loc, w_q, preferred_element_type=jnp.float32).astype(jnp.bfloat16)  27.3 us
    all_to_all x1, waiting for transfers between devices, device_step(): q_seq = lax.all_to_all(q_loc, 'sp', 1, 0, tiled=True)  11.3 us
    all_to_all x1, waiting for transfers between devices, device_step(): lax.all_to_all(attn_seq, 'sp', 0, 1, tiled=True)  10.4 us
    dot_general x1, matrix products, device_step(): jnp.dot(x_loc, w_k, preferred_element_type=jnp.float32).astype(jnp.bfloat16)  7.19 us
    dot_general x1, matrix products, device_step(): jnp.dot(x_loc, w_v, preferred_element_type=jnp.float32).astype(jnp.bfloat16)  6.89 us
  transfers between devices with their start and end apart: 4, of which 2 were waited for; matrix products, arithmetic and copies ran while one was open for 16% of the time, Pallas kernels for 0%

commit v1 on v0

v1 whole, which is shorter than its diff:
```python
import math
import jax
import jax.numpy as jnp
from jax import lax
from jax.experimental import pallas as pl
from jax.experimental.pallas import tpu as pltpu
from jax.sharding import PartitionSpec as P

MESH = pl.DeviceIdType.MESH
HEAD = 128
EXP_SCALE = math.log2(math.e) / math.sqrt(HEAD)
KC = 512
NC = 512
RING = 6
WO_BUFS = 4
AHEAD = 3
F32 = jnp.float32
BF16 = jnp.bfloat16


def block_kernel(x_ref, wq_ref, wk_ref, wv_ref, wo_ref, ids_ref, probs_ref,
                 h_ref, tab_ref,
                 xb, ring, wob, acc, kvacc, kv, ob, hb, oacc, mask, idsb, probsb, gsc, hsc, tabs,
                 ring_sem, wo_sem, loc_sem, xp_sem, xc_send, xc_recv, xr_send, xr_recv,
                 kv_sem, o_send, o_recv, hp_send, hp_recv, hc_send, hc_recv, hr_send, hr_recv,
                 t_send, t_recv, out_sem, tab_sem):
    tok, d = x_ref.shape
    own = 2 * tok
    rows = xb.shape[0]
    red = rows - own
    half = wq_ref.shape[1] // 2
    kvw = wk_ref.shape[1] // 2
    nk = d // KC
    per = half // (2 * kvw)
    n_kv = nk // per
    n_loads = n_kv + nk
    oh = d // 2
    nn = oh // NC
    groups = kvw // HEAD
    q_per = half // kvw
    gw = q_per * HEAD

    sp = lax.axis_index('sp')
    chip = sp // 2
    core = sp % 2
    partner = chip * 2 + (1 - core)
    across = (1 - chip) * 2 + core
    diag = (1 - chip) * 2 + (1 - core)

    def remote(src, dst, send, recv, dev):
        return pltpu.make_async_remote_copy(
            src_ref=src, dst_ref=dst, send_sem=send, recv_sem=recv,
            device_id={'sp': dev}, device_id_type=MESH)

    def load_kv(n):
        for j in range(per):
            r = pl.ds((n * per + j) * KC, KC)
            c = pl.ds(pl.multiple_of(core * kvw, HEAD), kvw)
            pltpu.make_async_copy(wk_ref.at[r, c], ring.at[n, :, pl.ds(2 * j * kvw, kvw)], ring_sem.at[n]).start()
            pltpu.make_async_copy(wv_ref.at[r, c], ring.at[n, :, pl.ds((2 * j + 1) * kvw, kvw)], ring_sem.at[n]).start()

    def load_q(n):
        slot = n % RING
        r = pl.ds(pl.multiple_of((n - n_kv) * KC, KC), KC)
        c = pl.ds(pl.multiple_of(core * half, HEAD), half)
        pltpu.make_async_copy(wq_ref.at[r, c], ring.at[slot], ring_sem.at[slot]).start()

    def wait_ring(slot):
        pltpu.make_async_copy(wq_ref.at[pl.ds(0, KC), pl.ds(0, half)], ring.at[slot], ring_sem.at[slot]).wait()

    def load_wo(n):
        slot = n % WO_BUFS
        c = pl.ds(pl.multiple_of(core * oh + n * NC, HEAD), NC)
        for side in range(2):
            r = pl.ds(pl.multiple_of((core if side == 0 else 1 - core) * half, HEAD), half)
            pltpu.make_async_copy(wo_ref.at[r, c], wob.at[slot, pl.ds(side * half, half), :], wo_sem.at[slot]).start()

    def wait_wo(slot):
        pltpu.make_async_copy(wo_ref.at[:, pl.ds(0, NC)], wob.at[slot], wo_sem.at[slot]).wait()

    own_rows = pl.ds(pl.multiple_of(core * tok, 16), tok)
    x_load = pltpu.make_async_copy(x_ref, xb.at[own_rows, :], loc_sem.at[0])
    ids_load = pltpu.make_async_copy(ids_ref, idsb, loc_sem.at[1])
    probs_load = pltpu.make_async_copy(probs_ref, probsb, loc_sem.at[2])
    x_load.start()
    ids_load.start()
    probs_load.start()
    for n in range(RING):
        if n < n_kv:
            load_kv(n)
        else:
            load_q(n)

    barrier = pltpu.get_barrier_semaphore()
    for dev in (partner, across, diag):
        pl.semaphore_signal(barrier, inc=1, device_id={'sp': dev}, device_id_type=MESH)
    pl.semaphore_wait(barrier, 3)

    x_load.wait()
    x_pair = remote(xb.at[own_rows, :], xb.at[own_rows, :], xp_sem.at[0], xp_sem.at[1], partner)
    x_pair.start()

    def x_cross(k):
        c = pl.ds(pl.multiple_of(k * KC, KC), KC)
        return remote(xb.at[pl.ds(0, red), c], xb.at[pl.ds(own, red), c], xc_send.at[k], xc_recv.at[k], across)

    def x_relay(k):
        c = pl.ds(pl.multiple_of(k * KC, KC), KC)
        part = xb.at[pl.ds(own, red), c]
        return remote(part, part, xr_send.at[k], xr_recv.at[k], partner)

    @pl.when(core == 0)
    def _():
        @pl.loop(0, nk)
        def _(k):
            x_cross(k).start()

    ids_load.wait()
    probs_load.wait()
    experts = probsb.shape[1]
    lane8 = lax.broadcasted_iota(jnp.int32, (tok, experts), 1)
    pr = probsb[...]
    hit0 = lane8 == idsb[:, 0:1]
    hit1 = lane8 == idsb[:, 1:2]
    p0 = jnp.sum(jnp.where(hit0, pr, 0.0), axis=1, keepdims=True)
    p1 = jnp.sum(jnp.where(hit1, pr, 0.0), axis=1, keepdims=True)
    hit = jnp.logical_or(hit0, hit1)
    gsc[...] = jnp.zeros_like(gsc)
    hsc[...] = jnp.zeros_like(hsc)
    gsc[0:tok, 0:experts] = jnp.where(hit, pr / (p0 + p1), 0.0)
    hsc[0:tok, 0:experts] = jnp.where(hit, 1.0, 0.0)
    mine = tabs.at[sp]
    tabs[sp, 0:experts, :] = jnp.transpose(gsc[...])[0:experts, :]
    tabs[sp, experts:2 * experts, :] = jnp.transpose(hsc[...])[0:experts, :]

    acc[...] = jnp.zeros_like(acc)
    kvacc[...] = jnp.zeros_like(kvacc)
    row = lax.broadcasted_iota(jnp.int32, (rows, 2 * own), 0)
    col = lax.broadcasted_iota(jnp.int32, (rows, 2 * own), 1)
    row_pos = jnp.where(row < own, row + chip * own, row - own + (1 - chip) * own)
    col_pos = jnp.where(col < own, col + chip * own, col - own + (1 - chip) * own)
    mask[...] = jnp.where(row_pos >= col_pos, 1.0, 0.0)

    tab_copies = [remote(mine, mine, t_send.at[i], t_recv.at[i], dev)
                  for i, dev in enumerate((partner, across, diag))]
    for copy in tab_copies:
        copy.start()

    x_pair.wait()

    @pl.loop(0, n_kv)
    def _(n):
        wait_ring(n)
        for j in range(per):
            c = pl.ds(pl.multiple_of((n * per + j) * KC, KC), KC)
            kvacc[...] += jnp.dot(xb[0:own, c], ring[n, :, 2 * j * kvw:2 * (j + 1) * kvw],
                                  preferred_element_type=F32)
        load_q(n + RING)

    kv[0:own, :] = kvacc[...].astype(BF16)

    for copy in tab_copies:
        copy.wait()
    tab_out = pltpu.make_async_copy(tabs, tab_ref, tab_sem)
    tab_out.start()

    kv_cross = remote(kv.at[pl.ds(0, own), :], kv.at[pl.ds(own, own), :], kv_sem.at[0], kv_sem.at[1], across)
    kv_cross.start()

    @pl.when(core == 0)
    def _():
        for k in range(AHEAD):
            x_cross(k).wait_recv()
            x_relay(k).start()

    @pl.loop(0, nk)
    def _(k):
        @pl.when(jnp.logical_and(core == 0, k + AHEAD < nk))
        def _():
            x_cross(k + AHEAD).wait_recv()
            x_relay(k + AHEAD).start()

        @pl.when(core == 1)
        def _():
            x_relay(k).wait_recv()

        n = n_kv + k
        slot = n % RING
        wait_ring(slot)
        c = pl.ds(pl.multiple_of(k * KC, KC), KC)
        acc[...] += jnp.dot(xb[:, c], ring[slot], preferred_element_type=F32)

        @pl.when(n + RING < n_loads)
        def _():
            load_q(n + RING)

        late = n + RING - n_loads
        for i, at in enumerate((0, 2, 4, 5)):
            @pl.when(late == at)
            def _():
                load_wo(i)

    kv_cross.wait()

    def o_pair(g):
        return remote(ob.at[:, pl.ds(pl.multiple_of(g * gw, HEAD), gw)],
                      ob.at[:, pl.ds(pl.multiple_of(half + g * gw, HEAD), gw)],
                      o_send.at[g], o_recv.at[g], partner)

    @pl.loop(0, groups)
    def _(g):
        kg = kv[:, pl.ds(pl.multiple_of(g * HEAD, HEAD), HEAD)]
        vg = kv[:, pl.ds(pl.multiple_of(kvw + g * HEAD, HEAD), HEAD)]
        for m in range(q_per):
            c = pl.ds(pl.multiple_of(g * gw + m * HEAD, HEAD), HEAD)
            s = lax.dot_general(acc[:, c].astype(BF16), kg, (((1,), (1,)), ((), ())),
                                preferred_element_type=F32)
            s = jnp.where(mask[...] > 0.5, s, -1e30)
            top = jnp.max(s, axis=1, keepdims=True)
            e = jnp.exp2((s - top) * EXP_SCALE)
            w = (e * (1.0 / jnp.sum(e, axis=1, keepdims=True))).astype(BF16)
            ob[:, c] = jnp.dot(w, vg, preferred_element_type=F32).astype(BF16)
        o_pair(g).start()

    def h_cols(side, n):
        return pl.ds(pl.multiple_of((core if side == 0 else 1 - core) * oh + n * NC, HEAD), NC)

    def h_pair(n):
        part = hb.at[pl.ds(0, rows), h_cols(0, n)]
        return remote(part, part, hp_send.at[n], hp_recv.at[n], partner)

    def h_cross(n):
        return remote(hb.at[pl.ds(red, own - red), h_cols(0, n)], hb.at[pl.ds(rows, own - red), h_cols(0, n)],
                      hc_send.at[n], hc_recv.at[n], across)

    def h_relay(n):
        part = hb.at[pl.ds(rows, own - red), h_cols(0, n)]
        return remote(part, part, hr_send.at[n], hr_recv.at[n], partner)

    def h_out(side, n):
        c = h_cols(side, n)
        return [pltpu.make_async_copy(
            hb.at[pl.ds(i * own, own), c],
            h_ref.at[pl.ds(pl.multiple_of((chip if i == 0 else 1 - chip) * own, 16), own), c],
            out_sem.at[side, n, i]) for i in range(2)]

    def relay_and_out(n):
        h_cross(n).wait_recv()
        h_relay(n).start()
        for copy in h_out(0, n):
            copy.start()

    def partner_out(n):
        h_pair(n).wait_recv()
        h_relay(n).wait_recv()
        for copy in h_out(1, n):
            copy.start()

    @pl.loop(0, nn)
    def _(n):
        slot = n % WO_BUFS
        wait_wo(slot)
        oacc[...] = jnp.dot(ob[:, 0:half], wob[slot, 0:half, :], preferred_element_type=F32)

        @pl.when(n == 0)
        def _():
            @pl.loop(0, groups)
            def _(g):
                o_pair(g).wait()

        part = oacc[...] + jnp.dot(ob[:, half:2 * half], wob[slot, half:2 * half, :], preferred_element_type=F32)
        hb[0:rows, h_cols(0, n)] = (xb[:, h_cols(0, n)].astype(F32) + part).astype(BF16)

        @pl.when(n + WO_BUFS < nn)
        def _():
            load_wo(n + WO_BUFS)

        h_cross(n).start()
        h_pair(n).start()

        @pl.when(n >= 2)
        def _():
            relay_and_out(n - 2)

        @pl.when(n >= 3)
        def _():
            partner_out(n - 3)

    relay_and_out(nn - 2)
    partner_out(nn - 3)
    relay_and_out(nn - 1)
    partner_out(nn - 2)
    partner_out(nn - 1)

    @pl.when(core == 0)
    def _():
        @pl.loop(0, nk)
        def _(k):
            x_cross(k).wait_send()
            x_relay(k).wait_send()

    @pl.loop(0, nn)
    def _(n):
        h_cross(n).wait_send()
        h_pair(n).wait_send()
        h_relay(n).wait_send()
        for side in range(2):
            for copy in h_out(side, n):
                copy.wait()

    tab_out.wait()


def dispatch_kernel(tab_ref, h_ref, hid_ref, buf_ref, pick, gate):
    sources, lines, lanes = tab_ref.shape
    experts = lines // 2
    tokens = h_ref.shape[0]
    tok = tokens // sources
    held = buf_ref.shape[0]
    sp = lax.axis_index('sp')

    @pl.when(pl.program_id(0) == 0)
    def _():
        before = lax.broadcasted_iota(jnp.int32, (lanes, lanes), 0) < lax.broadcasted_iota(jnp.int32, (lanes, lanes), 1)
        before = jnp.where(before, 1.0, 0.0).astype(BF16)
        dests, gates = [], []
        for s in range(sources):
            hits = tab_ref[s, experts:2 * experts, :]
            rank = jnp.dot(hits.astype(BF16), before, preferred_element_type=F32)
            dests.append(jnp.where(hits > 0.5, rank + (s * tok + 1.0), 0.0))
            gates.append(tab_ref[s, 0:experts, :])
        pair = lanes // tok
        line = lax.broadcasted_iota(jnp.int32, (experts, lanes), 0)
        slot = lax.broadcasted_iota(jnp.int32, (tokens, lanes), 0).astype(F32) + 1.0
        for e in range(held):
            total = jnp.zeros((tokens, 1), F32)
            for j in range(sources // pair):
                dest, g = dests[pair * j], gates[pair * j]
                for i in range(1, pair):
                    dest = dest + pltpu.roll(dests[pair * j + i], i * tok, 1)
                    g = g + pltpu.roll(gates[pair * j + i], i * tok, 1)
                mine = line == sp * held + e
                dest = jnp.sum(jnp.where(mine, dest, 0.0), axis=0, keepdims=True)
                g = jnp.sum(jnp.where(mine, g, 0.0), axis=0, keepdims=True)
                chosen = slot == dest
                pick[e * tokens:(e + 1) * tokens, j * lanes:(j + 1) * lanes] = jnp.where(chosen, 1.0, 0.0).astype(BF16)
                total = total + jnp.sum(jnp.where(chosen, g, 0.0), axis=1, keepdims=True)
            gate[e * tokens:(e + 1) * tokens, :] = total

    hid_ref[...] = h_ref[pl.ds(pl.multiple_of(sp * tok, 16), tok), :]
    for e in range(held):
        r = slice(e * tokens, (e + 1) * tokens)
        y = jnp.dot(pick[r, :], h_ref[...], preferred_element_type=F32)
        buf_ref[e] = (gate[r, :] * y).astype(BF16)


def solution(mesh):
    row_spec = P(('dp', 'sp'), None)
    buf_spec = P(('dp', 'sp'), None, None)
    group = mesh.shape['sp']

    def device_step(x, w_q, w_k, w_v, w_o, ids, probs):
        tok, d = x.shape
        half, kvw, oh = w_q.shape[1] // 2, w_k.shape[1] // 2, d // 2
        experts = probs.shape[1]
        own, tokens = 2 * tok, group * tok
        rows = own + tok
        nk, nn = d // KC, oh // NC
        any_spec = pl.BlockSpec(memory_space=pl.ANY)
        dma = pltpu.SemaphoreType.DMA
        h, tab = pl.pallas_call(
            block_kernel,
            out_shape=(jax.ShapeDtypeStruct((tokens, d), BF16),
                       jax.ShapeDtypeStruct((group, 2 * experts, 128), F32)),
            in_specs=[any_spec] * 7,
            out_specs=(any_spec, any_spec),
            scratch_shapes=[
                pltpu.VMEM((rows, d), BF16),
                pltpu.VMEM((RING, KC, half), BF16),
                pltpu.VMEM((WO_BUFS, d, NC), BF16),
                pltpu.VMEM((rows, half), F32),
                pltpu.VMEM((own, 2 * kvw), F32),
                pltpu.VMEM((tokens, 2 * kvw), BF16),
                pltpu.VMEM((rows, 2 * half), BF16),
                pltpu.VMEM((tokens, d), BF16),
                pltpu.VMEM((rows, NC), F32),
                pltpu.VMEM((rows, tokens), F32),
                pltpu.VMEM((tok, 2), jnp.int32),
                pltpu.VMEM((tok, experts), F32),
                pltpu.VMEM((128, 128), F32),
                pltpu.VMEM((128, 128), F32),
                pltpu.VMEM((group, 2 * experts, 128), F32),
                dma((RING,)), dma((WO_BUFS,)), dma((3,)), dma((2,)),
                dma((nk,)), dma((nk,)), dma((nk,)), dma((nk,)),
                dma((2,)), dma((kvw // HEAD,)), dma((kvw // HEAD,)),
                dma((nn,)), dma((nn,)), dma((nn,)), dma((nn,)), dma((nn,)), dma((nn,)),
                dma((3,)), dma((3,)), dma((2, nn, 2)), dma(()),
            ],
            compiler_params=pltpu.CompilerParams(
                collective_id=0, has_side_effects=True, vmem_limit_bytes=66_000_000),
            name='block',
        )(x, w_q, w_k, w_v, w_o, ids, probs)
        wide = 1024
        return pl.pallas_call(
            dispatch_kernel,
            grid=(d // wide,),
            out_shape=(jax.ShapeDtypeStruct((tok, d), BF16),
                       jax.ShapeDtypeStruct((experts // group, tokens, d), BF16)),
            in_specs=[pl.BlockSpec((group, 2 * experts, 128), lambda i: (0, 0, 0)),
                      pl.BlockSpec((tokens, wide), lambda i: (0, i))],
            out_specs=(pl.BlockSpec((tok, wide), lambda i: (0, i)),
                       pl.BlockSpec((experts // group, tokens, wide), lambda i: (0, 0, i))),
            scratch_shapes=[pltpu.VMEM((experts // group * tokens, tokens), BF16),
                            pltpu.VMEM((experts // group * tokens, 1), F32)],
            name='dispatch',
        )(tab, h)

    return jax.shard_map(device_step, mesh=mesh,
                         in_specs=(row_spec, P(), P(), P(), P(), row_spec, row_spec),
                         out_specs=(row_spec, buf_spec), check_vma=False)
```

time: 251 us -> 60.8 us (0.24)
  matrix products: 75.3 us -> 0 us
  blocking collectives: 74.3 us -> 0 us
  local copies, waits for them, and re-layouts: 60 us -> 2.77 us
  Pallas kernels: 0 us -> 57 us
  waiting for transfers between devices: 21.7 us -> 0 us
  starting transfers between devices: 15.1 us -> 0 us
  other arithmetic: 2.83 us -> 0 us
    all_to_all x1 -> x0, blocking collectives: 74.3 us -> none  [device_step(): recv_buf = lax.all_to_all(send_buf, 'sp', 0, 1, tiled=True)]
    dot_general x5 -> x0, matrix products: 72.5 us -> none  [the longest x1 28.8 us: device_step(): out_proj = jnp.dot(attn_loc, w_o, preferred_element_type=jnp.float32)]
    pallas_call x0 -> x2, Pallas kernels: none -> 57 us  [the longest x1 49.6 us: device_step(): pl.pallas_call(block_kernel, out_shape=(jax.ShapeDtypeStruct((tokens, d),...]
    scatter x1 -> x0, local copies, waits for them, and re-layouts: 44.4 us -> none  [route_rows(): return send_buf.at[expert_ids, slot_rank].set(gated, unique_indices=True)]
    all_to_all x4 -> x0, waiting for transfers between devices: 21.7 us -> none  [the longest x1 11.3 us: device_step(): q_seq = lax.all_to_all(q_loc, 'sp', 1, 0, tiled=True)]
    all_to_all x4 -> x0, starting transfers between devices: 15.1 us -> none  [the longest x1 4.61 us: device_step(): k_seq = lax.all_to_all(k_loc, 'sp', 1, 0, tiled=True)]
    all_to_all x5 -> x0, local copies, waits for them, and re-layouts: 3.5 us -> none  [the longest x1 3.11 us: device_step(): recv_buf = lax.all_to_all(send_buf, 'sp', 0, 1, tiled=True)]
    broadcast_in_dim x1 -> x0, local copies, waits for them, and re-layouts: 3.47 us -> none  [route_rows(): send_buf = jnp.zeros((experts, tok_dev, width), jnp.bfloat16)]
  transfers between devices with their start and end apart: 4 -> 0, of which waited for: 2 -> 0; matrix products, arithmetic and copies ran while one was open for 16% -> 0% of each run, Pallas kernels for 0% -> 0%
where the time goes in v1:
time: 60.8 us; the launch traced here: 60.4 us
  Pallas kernels  57 us (94%)
  local copies, waits for them, and re-layouts  2.77 us (5%)
  between operations  0.64 us (1%)
    pallas_call x1, Pallas kernels, device_step(): pl.pallas_call(block_kernel, out_shape=(jax.ShapeDtypeStruct((tokens, d),...  49.6 us
    pallas_call x1, Pallas kernels, device_step(): pl.pallas_call(dispatch_kernel, grid=(d // wide,), out_shape=(jax.ShapeDt...  7.32 us
    unnamed x2, local copies, waits for them, and re-layouts  2.77 us

profile of v1, /device:TPU:0, one launch (start us, length us, event | category | flops | bytes accessed | tf_op | source)
XLA Modules:
  0.0 60.4 jit_solution(9713478474559081580)
XLA Ops:
  0.6 1.4 %copy.9.ids_ref = s32[64,2]{1,0:T(8,128)} copy(s32[64,2]{0,1:T(2,128)} %param.12) | data formatting | bytes 1024 | tf_op args[5]
  2.0 1.4 %copy.10.probs_ref = f32[64,8]{1,0:T(8,128)} copy(f32[64,8]{0,1:T(8,128)} %param.13) | data formatting | bytes 4096 | tf_op args[6]
  3.4 49.6 %block.1 = (bf16[256,6144]{1,0:T(8,128)(2,1)}, f32[4,16,128]{2,1,0:T(8,128)}) custom-call(bf16[64,6144]{1,0:T(8,128)(2,1)} %x_ref.1, bf16[6144,6144]{1,0:T(8,128)(2,1)} %wq_ref.1, bf16[6144,1024]{1,0:T(8,128)(2,1)} %wk_ref.1, bf16[6144,1024]{1,0:T(8,128)(2,1)} %wv_ref.1, bf16[6144,6144]{1,0:T(8,128)(2,1)} %wo_ref.1, s32[64,2]{1,0:T(8,128)} %copy.9.ids_ref, ...), custom_call_target="tpu_custom_call" | custom-call | tf_op jit(solution)/shard_map/block/pallas_call | solution.py:371
  53.0 7.3 %dispatch.1 = (bf16[64,6144]{1,0:T(8,128)(2,1)}, bf16[2,256,6144]{2,1,0:T(8,128)(2,1)}) custom-call(f32[4,16,128]{2,1,0:T(8,128)} %get-tuple-element.4.tab_ref, bf16[256,6144]{1,0:T(8,128)(2,1)} %get-tuple-element.5.h_ref), custom_call_target="tpu_custom_call" | custom-call | tf_op jit(solution)/shard_map/dispatch/pallas_call | solution.py:404

commit v2 on v1

v2 whole, which is shorter than its diff:
```python
import math
import jax
import jax.numpy as jnp
from jax import lax
from jax.experimental import pallas as pl
from jax.experimental.pallas import tpu as pltpu
from jax.sharding import PartitionSpec as P

MESH = pl.DeviceIdType.MESH
HEAD = 128
SCALE = 1.0 / math.sqrt(HEAD)
EXP_SCALE = math.log2(math.e) * SCALE
MASKED = -1e30 / SCALE
KC = 1024
NC = 512
RING = 3
WO_BUFS = 4
AHEAD = 2
EARLY = 2
BLOCK_VMEM = 60_000_000
OUT_SPACE = pltpu.VMEM
F32 = jnp.float32
BF16 = jnp.bfloat16


def block_kernel(x_ref, wq_ref, wk_ref, wv_ref, wo_ref, ids_ref, probs_ref,
                 h_ref, pick_ref, gate_ref,
                 xb, ring, wob, acc, kvacc, kv, ob, oacc, mask, idsb, probsb, tabs,
                 ring_sem, wo_sem, loc_sem, xp_sem, xc_send, xc_recv, xr_send, xr_recv,
                 kv_sem, o_send, o_recv, hp_send, hp_recv, hc_send, hc_recv, hr_send, hr_recv,
                 t_send, t_recv):
    tok, d = x_ref.shape
    own = 2 * tok
    rows = xb.shape[0]
    red = rows - own
    half = wq_ref.shape[1] // 2
    kvw = wk_ref.shape[1] // 2
    nk = d // KC
    per = half // (2 * kvw)
    n_kv = nk // per
    n_loads = n_kv + nk
    oh = d // 2
    nn = oh // NC
    groups = kvw // HEAD
    q_per = half // kvw
    gw = q_per * HEAD

    sp = lax.axis_index('sp')
    chip = sp // 2
    core = sp % 2
    partner = chip * 2 + (1 - core)
    across = (1 - chip) * 2 + core
    diag = (1 - chip) * 2 + (1 - core)

    def remote(src, dst, send, recv, dev):
        return pltpu.make_async_remote_copy(
            src_ref=src, dst_ref=dst, send_sem=send, recv_sem=recv,
            device_id={'sp': dev}, device_id_type=MESH)

    def load_kv(n):
        for j in range(per):
            r = pl.ds((n * per + j) * KC, KC)
            c = pl.ds(pl.multiple_of(core * kvw, HEAD), kvw)
            pltpu.make_async_copy(wk_ref.at[r, c], ring.at[n, :, pl.ds(2 * j * kvw, kvw)], ring_sem.at[n]).start()
            pltpu.make_async_copy(wv_ref.at[r, c], ring.at[n, :, pl.ds((2 * j + 1) * kvw, kvw)], ring_sem.at[n]).start()

    def load_q(n):
        slot = n % RING
        r = pl.ds(pl.multiple_of((n - n_kv) * KC, KC), KC)
        c = pl.ds(pl.multiple_of(core * half, HEAD), half)
        pltpu.make_async_copy(wq_ref.at[r, c], ring.at[slot], ring_sem.at[slot]).start()

    def wait_ring(slot):
        pltpu.make_async_copy(wq_ref.at[pl.ds(0, KC), pl.ds(0, half)], ring.at[slot], ring_sem.at[slot]).wait()

    def load_wo(n):
        slot = n % WO_BUFS
        c = pl.ds(pl.multiple_of(core * oh + n * NC, HEAD), NC)
        for side in range(2):
            r = pl.ds(pl.multiple_of((core if side == 0 else 1 - core) * half, HEAD), half)
            pltpu.make_async_copy(wo_ref.at[r, c], wob.at[slot, pl.ds(side * half, half), :], wo_sem.at[slot]).start()

    def wait_wo(slot):
        pltpu.make_async_copy(wo_ref.at[:, pl.ds(0, NC)], wob.at[slot], wo_sem.at[slot]).wait()

    own_rows = pl.ds(pl.multiple_of(core * tok, 16), tok)
    x_load = pltpu.make_async_copy(x_ref, xb.at[own_rows, :], loc_sem.at[0])
    ids_load = pltpu.make_async_copy(ids_ref, idsb, loc_sem.at[1])
    probs_load = pltpu.make_async_copy(probs_ref, probsb, loc_sem.at[2])
    x_load.start()
    ids_load.start()
    probs_load.start()
    barrier = pltpu.get_barrier_semaphore()
    for dev in (partner, across, diag):
        pl.semaphore_signal(barrier, inc=1, device_id={'sp': dev}, device_id_type=MESH)
    with jax.named_scope('xl'):
        x_load.wait()
    for n in range(RING):
        if n < n_kv:
            load_kv(n)
        else:
            load_q(n)
    with jax.named_scope('bar'):
        pl.semaphore_wait(barrier, 3)

    x_pair = remote(xb.at[own_rows, :], xb.at[own_rows, :], xp_sem.at[0], xp_sem.at[1], partner)
    x_pair.start()

    def x_cross(k):
        c = pl.ds(pl.multiple_of(k * KC, KC), KC)
        return remote(xb.at[pl.ds(0, red), c], xb.at[pl.ds(own, red), c], xc_send.at[k], xc_recv.at[k], across)

    def x_relay(k):
        c = pl.ds(pl.multiple_of(k * KC, KC), KC)
        part = xb.at[pl.ds(own, red), c]
        return remote(part, part, xr_send.at[k], xr_recv.at[k], partner)

    @pl.when(core == 0)
    def _():
        for k in range(nk):
            x_cross(k).start()

    acc[...] = jnp.zeros_like(acc)
    kvacc[...] = jnp.zeros_like(kvacc)
    key = lax.broadcasted_iota(jnp.int32, (2 * own, 2 * own), 0)
    que = lax.broadcasted_iota(jnp.int32, (2 * own, 2 * own), 1)
    que = jnp.where(que < own, que, own + que % red)
    key_pos = jnp.where(key < own, key + chip * own, key - chip * own)
    que_pos = jnp.where(que < own, que + chip * own, que - chip * own)
    mask[...] = jnp.where(que_pos >= key_pos, 1.0, 0.0)
    ids_load.wait()
    probs_load.wait()
    experts = probsb.shape[0]
    line = lax.broadcasted_iota(jnp.int32, (experts, tok), 0)
    pr = probsb[...]
    hit0 = line == idsb[0:1, :]
    hit1 = line == idsb[1:2, :]
    p0 = jnp.sum(jnp.where(hit0, pr, 0.0), axis=0, keepdims=True)
    p1 = jnp.sum(jnp.where(hit1, pr, 0.0), axis=0, keepdims=True)
    hit = jnp.logical_or(hit0, hit1)
    tabs[sp] = jnp.zeros(tabs.shape[1:], F32)
    tabs[sp, 0:experts, 0:tok] = jnp.where(hit, pr / (p0 + p1), 0.0)
    tabs[sp, experts:2 * experts, 0:tok] = jnp.where(hit, 1.0, 0.0)

    with jax.named_scope('wxp'):
        x_pair.wait()

    @pl.loop(0, n_kv)
    def _(n):
        with jax.named_scope('wkv'):
            wait_ring(n)
        for j in range(per):
            c = pl.ds(pl.multiple_of((n * per + j) * KC, KC), KC)
            kvacc[...] += jnp.dot(xb[0:own, c], ring[n, :, 2 * j * kvw:2 * (j + 1) * kvw],
                                  preferred_element_type=F32)
        load_q(n + RING)

    kv[0:own, :] = kvacc[...].astype(BF16)
    kv_cross = remote(kv.at[pl.ds(0, own), :], kv.at[pl.ds(own, own), :], kv_sem.at[0], kv_sem.at[1], across)
    kv_cross.start()
    mine = tabs.at[sp]
    tab_copies = [remote(mine, mine, t_send.at[i], t_recv.at[i], dev)
                  for i, dev in enumerate((partner, across, diag))]
    for copy in tab_copies:
        copy.start()

    @pl.when(core == 0)
    def _():
        for k in range(AHEAD):
            with jax.named_scope('wxc0'):
                x_cross(k).wait_recv()
            x_relay(k).start()

    @pl.loop(0, nk)
    def _(k):
        @pl.when(jnp.logical_and(core == 0, k + AHEAD < nk))
        def _():
            with jax.named_scope('wxc'):
                x_cross(k + AHEAD).wait_recv()
            x_relay(k + AHEAD).start()

        @pl.when(core == 1)
        def _():
            with jax.named_scope('wxr'):
                x_relay(k).wait_recv()

        n = n_kv + k
        slot = n % RING
        with jax.named_scope('wq'):
            wait_ring(slot)
        c = pl.ds(pl.multiple_of(k * KC, KC), KC)
        acc[...] += jnp.dot(xb[:, c], ring[slot], preferred_element_type=F32)

        @pl.when(n + RING < n_loads)
        def _():
            load_q(n + RING)

        late = n + RING - n_loads
        for i, at in enumerate((0, 1, 2, 2)):
            @pl.when(late == at)
            def _():
                load_wo(i)

    with jax.named_scope('wkvx'):
        kv_cross.wait()

    def o_pair(g):
        return remote(ob.at[:, pl.ds(pl.multiple_of(g * gw, HEAD), gw)],
                      ob.at[:, pl.ds(pl.multiple_of(half + g * gw, HEAD), gw)],
                      o_send.at[g], o_recv.at[g], partner)

    @pl.loop(0, groups)
    def _(g):
        kg = kv[:, pl.ds(pl.multiple_of(g * HEAD, HEAD), HEAD)]
        vt = jnp.transpose(kv[:, pl.ds(pl.multiple_of(kvw + g * HEAD, HEAD), HEAD)])
        cols = [pl.ds(pl.multiple_of(g * gw + m * HEAD, HEAD), HEAD) for m in range(q_per)]
        q = jnp.concatenate([acc[0:own, c].astype(BF16) for c in cols]
                            + [acc[own:rows, c].astype(BF16) for c in cols], axis=0)
        seen = jnp.concatenate([mask[:, 0:own]] * q_per + [mask[:, own:2 * own]] * (q_per * red // own), axis=1)
        s = lax.dot_general(kg, q, (((1,), (1,)), ((), ())), preferred_element_type=F32)
        s = jnp.where(seen > 0.5, s, MASKED)
        top = jnp.max(s, axis=0, keepdims=True)
        e = jnp.exp2((s - top) * EXP_SCALE)
        w = (e * (1.0 / jnp.sum(e, axis=0, keepdims=True))).astype(BF16)
        o = jnp.transpose(jnp.dot(vt, w, preferred_element_type=F32)).astype(BF16)
        for m, c in enumerate(cols):
            ob[0:own, c] = o[m * own:(m + 1) * own, :]
            ob[own:rows, c] = o[q_per * own + m * red:q_per * own + (m + 1) * red, :]
        with jax.named_scope('os'):
            o_pair(g).start()

    def h_cols(side, n):
        return pl.ds(pl.multiple_of((core if side == 0 else 1 - core) * oh + n * NC, HEAD), NC)

    def h_pair(n):
        part = h_ref.at[pl.ds(0, rows), h_cols(0, n)]
        return remote(part, part, hp_send.at[n], hp_recv.at[n], partner)

    def h_cross(n):
        return remote(h_ref.at[pl.ds(red, own - red), h_cols(0, n)], h_ref.at[pl.ds(rows, own - red), h_cols(0, n)],
                      hc_send.at[n], hc_recv.at[n], across)

    def h_relay(n):
        part = h_ref.at[pl.ds(rows, own - red), h_cols(0, n)]
        return remote(part, part, hr_send.at[n], hr_recv.at[n], partner)

    def relay(n):
        with jax.named_scope('whc'):
            h_cross(n).wait_recv()
        h_relay(n).start()

    def finish(n, total):
        h_ref[0:rows, h_cols(0, n)] = (xb[:, h_cols(0, n)].astype(F32) + total).astype(BF16)

        @pl.when(n + WO_BUFS < nn)
        def _():
            load_wo(n + WO_BUFS)

        h_cross(n).start()
        h_pair(n).start()

    for n in range(EARLY):
        wait_wo(n)
        oacc[n] = jnp.dot(ob[:, 0:half], wob[n, 0:half, :], preferred_element_type=F32)

    with jax.named_scope('tab'):
        for copy in tab_copies:
            copy.wait()
    lanes = tabs.shape[2]
    held = pick_ref.shape[0] // pick_ref.shape[1]
    tokens = pick_ref.shape[1]
    before = lax.broadcasted_iota(jnp.int32, (lanes, lanes), 0) < lax.broadcasted_iota(jnp.int32, (lanes, lanes), 1)
    before = jnp.where(before, 1.0, 0.0).astype(BF16)
    dests, gates = [], []
    for j in range(2):
        dest, g = 0.0, 0.0
        for i in range(2):
            s = (chip if j == 0 else 1 - chip) * 2 + i
            hits = tabs[s, experts:2 * experts, :]
            rank = jnp.dot(hits.astype(BF16), before, preferred_element_type=F32)
            at = jnp.where(hits > 0.5, rank + (s * tok + 1).astype(F32), 0.0)
            gs = tabs[s, 0:experts, :]
            dest = dest + (at if i == 0 else pltpu.roll(at, tok, 1))
            g = g + (gs if i == 0 else pltpu.roll(gs, tok, 1))
        dests.append(dest)
        gates.append(g)
    line = lax.broadcasted_iota(jnp.int32, (experts, lanes), 0)
    slot = lax.broadcasted_iota(jnp.int32, (tokens, lanes), 0).astype(F32) + 1.0
    for e in range(held):
        total = jnp.zeros((tokens, 1), F32)
        for j in range(2):
            here = line == sp * held + e
            dest = jnp.sum(jnp.where(here, dests[j], 0.0), axis=0, keepdims=True)
            g = jnp.sum(jnp.where(here, gates[j], 0.0), axis=0, keepdims=True)
            chosen = slot == dest
            pick_ref[e * tokens:(e + 1) * tokens, j * lanes:(j + 1) * lanes] = jnp.where(chosen, 1.0, 0.0).astype(BF16)
            total = total + jnp.sum(jnp.where(chosen, g, 0.0), axis=1, keepdims=True)
        gate_ref[e * tokens:(e + 1) * tokens, :] = jnp.broadcast_to(total, (tokens, lanes))

    with jax.named_scope('wo'):
        @pl.loop(0, groups)
        def _(g):
            o_pair(g).wait()

    for n in range(EARLY):
        finish(n, oacc[n] + jnp.dot(ob[:, half:2 * half], wob[n, half:2 * half, :], preferred_element_type=F32))

    @pl.loop(EARLY, nn)
    def _(n):
        slot = n % WO_BUFS
        with jax.named_scope('wwo'):
            wait_wo(slot)
        finish(n, jnp.dot(ob[...], wob[slot], preferred_element_type=F32))
        relay(n - 2)

    relay(nn - 2)
    relay(nn - 1)

    @pl.when(core == 0)
    def _():
        @pl.loop(0, nk)
        def _(k):
            x_cross(k).wait_send()
            x_relay(k).wait_send()

    with jax.named_scope('end'):
        @pl.loop(0, nn)
        def _(n):
            h_cross(n).wait_send()
            h_pair(n).wait()
            h_relay(n).wait()


def dispatch_kernel(pick_ref, gate_ref, h_ref, hid_ref, buf_ref):
    tok, wide = hid_ref.shape
    held, tokens = buf_ref.shape[0], buf_ref.shape[1]
    core = lax.axis_index('sp') % 2
    c = pl.ds(pl.multiple_of(pl.program_id(0) * wide, wide), wide)
    hid_ref[...] = h_ref[pl.ds(pl.multiple_of(core * tok, 16), tok), c]
    for e in range(held):
        r = slice(e * tokens, (e + 1) * tokens)
        y = jnp.dot(pick_ref[r, :], h_ref[:, c], preferred_element_type=F32)
        g = gate_ref[r, :]
        for j in range(0, wide, HEAD):
            buf_ref[e, :, j:j + HEAD] = (g * y[:, j:j + HEAD]).astype(BF16)


def solution(mesh):
    row_spec = P(('dp', 'sp'), None)
    buf_spec = P(('dp', 'sp'), None, None)
    group = mesh.shape['sp']

    def device_step(x, w_q, w_k, w_v, w_o, ids, probs):
        tok, d = x.shape
        half, kvw, oh = w_q.shape[1] // 2, w_k.shape[1] // 2, d // 2
        experts = probs.shape[1]
        held = experts // group
        own, tokens = 2 * tok, group * tok
        rows = own + tok
        nk, nn = d // KC, oh // NC
        any_spec = pl.BlockSpec(memory_space=pl.ANY)
        vmem_spec = pl.BlockSpec(memory_space=pltpu.VMEM)
        dma = pltpu.SemaphoreType.DMA
        h, pick, gate = pl.pallas_call(
            block_kernel,
            out_shape=(OUT_SPACE((tokens, d), BF16),
                       OUT_SPACE((held * tokens, tokens), BF16),
                       OUT_SPACE((held * tokens, 128), F32)),
            in_specs=[any_spec] * 7,
            out_specs=(vmem_spec,) * 3,
            scratch_shapes=[
                pltpu.VMEM((rows, d), BF16),
                pltpu.VMEM((RING, KC, half), BF16),
                pltpu.VMEM((WO_BUFS, d, NC), BF16),
                pltpu.VMEM((rows, half), F32),
                pltpu.VMEM((own, 2 * kvw), F32),
                pltpu.VMEM((tokens, 2 * kvw), BF16),
                pltpu.VMEM((rows, 2 * half), BF16),
                pltpu.VMEM((EARLY, rows, NC), F32),
                pltpu.VMEM((tokens, tokens), F32),
                pltpu.VMEM((2, tok), jnp.int32),
                pltpu.VMEM((experts, tok), F32),
                pltpu.VMEM((group, 2 * experts, 128), F32),
                dma((RING,)), dma((WO_BUFS,)), dma((3,)), dma((2,)),
                dma((nk,)), dma((nk,)), dma((nk,)), dma((nk,)),
                dma((2,)), dma((kvw // HEAD,)), dma((kvw // HEAD,)),
                dma((nn,)), dma((nn,)), dma((nn,)), dma((nn,)), dma((nn,)), dma((nn,)),
                dma((3,)), dma((3,)),
            ],
            compiler_params=pltpu.CompilerParams(
                collective_id=0, has_side_effects=True, vmem_limit_bytes=BLOCK_VMEM),
            name='block',
        )(x, w_q, w_k, w_v, w_o, ids.T, probs.T)
        wide = 1024
        return pl.pallas_call(
            dispatch_kernel,
            grid=(d // wide,),
            out_shape=(jax.ShapeDtypeStruct((tok, d), BF16),
                       jax.ShapeDtypeStruct((held, tokens, d), BF16)),
            in_specs=[vmem_spec] * 3,
            out_specs=(pl.BlockSpec((tok, wide), lambda i: (0, i)),
                       pl.BlockSpec((held, tokens, wide), lambda i: (0, 0, i))),
            compiler_params=pltpu.CompilerParams(vmem_limit_bytes=16_000_000),
            name='dispatch',
        )(pick, gate, h)

    return jax.shard_map(device_step, mesh=mesh,
                         in_specs=(row_spec, P(), P(), P(), P(), row_spec, row_spec),
                         out_specs=(row_spec, buf_spec), check_vma=False)
```

time: 60.8 us -> 46.3 us (0.76)
  Pallas kernels: 57 us -> 45.6 us
  local copies, waits for them, and re-layouts: 2.77 us -> 0 us
    pallas_call x1, Pallas kernels: 49.6 us -> 40.8 us  [device_step(): pl.pallas_call(block_kernel, out_shape=(OUT_SPACE((tokens, d), BF16), OUT...]
    unnamed x2 -> x0, local copies, waits for them, and re-layouts: 2.77 us -> none
    pallas_call x1, Pallas kernels: 7.32 us -> 4.72 us  [device_step(): pl.pallas_call(dispatch_kernel, grid=(d // wide,), out_shape=(jax.ShapeDt...]
where the time goes in v2:
time: 46.3 us; the launch traced here: 46.2 us
  Pallas kernels  45.6 us (98%)
  between operations  0.64 us (1%)
    pallas_call x1, Pallas kernels, device_step(): pl.pallas_call(block_kernel, out_shape=(OUT_SPACE((tokens, d), BF16), OUT...  40.8 us
    pallas_call x1, Pallas kernels, device_step(): pl.pallas_call(dispatch_kernel, grid=(d // wide,), out_shape=(jax.ShapeDt...  4.72 us

profile of v2, /device:TPU:0, one launch (start us, length us, event | category | flops | bytes accessed | tf_op | source)
XLA Modules:
  0.0 46.2 jit_solution(12666618458912866299)
XLA Ops:
  0.6 40.8 %block.1 = (bf16[256,6144]{1,0:T(8,128)(2,1)S(1)}, bf16[512,256]{1,0:T(8,128)(2,1)S(1)}, f32[512,128]{1,0:T(8,128)S(1)}) custom-call(bf16[64,6144]{1,0:T(8,128)(2,1)} %x_ref.1, bf16[6144,6144]{1,0:T(8,128)(2,1)} %wq_ref.1, bf16[6144,1024]{1,0:T(8,128)(2,1)} %wk_ref.1, bf16[6144,1024]{1,0:T(8,128)(2,1)} %wv_ref.1, bf16[6144,6144]{1,0:T(8,128)(2,1)} %wo_ref.1, ...), custom_call_target="tpu_custom_call" | custom-call | tf_op jit(solution)/shard_map/block/pallas_call | solution.py:364
  41.5 4.7 %dispatch.1 = (bf16[64,6144]{1,0:T(8,128)(2,1)}, bf16[2,256,6144]{2,1,0:T(8,128)(2,1)}) custom-call(bf16[512,256]{1,0:T(8,128)(2,1)S(1)} %get-tuple-element.5.pick_ref, f32[512,128]{1,0:T(8,128)S(1)} %get-tuple-element.6.gate_ref, bf16[256,6144]{1,0:T(8,128)(2,1)S(1)} %get-tuple-element.7.h_ref), custom_call_target="tpu_custom_call" | custom-call | tf_op jit(solution)/shard_map/dispatch/pallas_call | solution.py:395

commit v3 on v2

--- a/solution.py
+++ b/solution.py
@@ -17,7 +17,11 @@
 WO_BUFS = 4
 AHEAD = 2
 EARLY = 2
-BLOCK_VMEM = 60_000_000
+LAG = 3
+KV_STEP = 3
+PICK_STEP = 1
+WIDE = 512
+BLOCK_VMEM = 59_000_000
 OUT_SPACE = pltpu.VMEM
 F32 = jnp.float32
 BF16 = jnp.bfloat16
@@ -25,7 +29,7 @@
 
 def block_kernel(x_ref, wq_ref, wk_ref, wv_ref, wo_ref, ids_ref, probs_ref,
                  h_ref, pick_ref, gate_ref,
-                 xb, ring, wob, acc, kvacc, kv, ob, oacc, mask, idsb, probsb, tabs,
+                 xb, ring, wob, acc, kvacc, kv, ob, oacc, idsb, probsb, tabs,
                  ring_sem, wo_sem, loc_sem, xp_sem, xc_send, xc_recv, xr_send, xr_recv,
                  kv_sem, o_send, o_recv, hp_send, hp_recv, hc_send, hc_recv, hr_send, hr_recv,
                  t_send, t_recv):
@@ -85,17 +89,20 @@
 
     own_rows = pl.ds(pl.multiple_of(core * tok, 16), tok)
     x_load = pltpu.make_async_copy(x_ref, xb.at[own_rows, :], loc_sem.at[0])
+    for k in range(nk):
+        c = pl.ds(k * KC, KC)
+        pltpu.make_async_copy(x_ref.at[:, c], xb.at[own_rows, c], loc_sem.at[0]).start()
     ids_load = pltpu.make_async_copy(ids_ref, idsb, loc_sem.at[1])
     probs_load = pltpu.make_async_copy(probs_ref, probsb, loc_sem.at[2])
-    x_load.start()
     ids_load.start()
     probs_load.start()
+    load_kv(0)
     barrier = pltpu.get_barrier_semaphore()
     for dev in (partner, across, diag):
         pl.semaphore_signal(barrier, inc=1, device_id={'sp': dev}, device_id_type=MESH)
     with jax.named_scope('xl'):
         x_load.wait()
-    for n in range(RING):
+    for n in range(1, RING):
         if n < n_kv:
             load_kv(n)
         else:
@@ -115,19 +122,6 @@
         part = xb.at[pl.ds(own, red), c]
         return remote(part, part, xr_send.at[k], xr_recv.at[k], partner)
 
-    @pl.when(core == 0)
-    def _():
-        for k in range(nk):
-            x_cross(k).start()
-
-    acc[...] = jnp.zeros_like(acc)
-    kvacc[...] = jnp.zeros_like(kvacc)
-    key = lax.broadcasted_iota(jnp.int32, (2 * own, 2 * own), 0)
-    que = lax.broadcasted_iota(jnp.int32, (2 * own, 2 * own), 1)
-    que = jnp.where(que < own, que, own + que % red)
-    key_pos = jnp.where(key < own, key + chip * own, key - chip * own)
-    que_pos = jnp.where(que < own, que + chip * own, que - chip * own)
-    mask[...] = jnp.where(que_pos >= key_pos, 1.0, 0.0)
     ids_load.wait()
     probs_load.wait()
     experts = probsb.shape[0]
@@ -141,6 +135,19 @@
     tabs[sp] = jnp.zeros(tabs.shape[1:], F32)
     tabs[sp, 0:experts, 0:tok] = jnp.where(hit, pr / (p0 + p1), 0.0)
     tabs[sp, experts:2 * experts, 0:tok] = jnp.where(hit, 1.0, 0.0)
+    mine = tabs.at[sp]
+    tab_copies = [remote(mine, mine, t_send.at[i], t_recv.at[i], dev)
+                  for i, dev in enumerate((partner, across, diag))]
+    for copy in tab_copies:
+        copy.start()
+
+    @pl.when(core == 0)
+    def _():
+        for k in range(nk):
+            x_cross(k).start()
+
+    acc[...] = jnp.zeros_like(acc)
+    kvacc[...] = jnp.zeros_like(kvacc)
 
     with jax.named_scope('wxp'):
         x_pair.wait()
@@ -156,16 +163,59 @@
         load_q(n + RING)
 
     kv[0:own, :] = kvacc[...].astype(BF16)
-    kv_cross = remote(kv.at[pl.ds(0, own), :], kv.at[pl.ds(own, own), :], kv_sem.at[0], kv_sem.at[1], across)
-    kv_cross.start()
-    mine = tabs.at[sp]
-    tab_copies = [remote(mine, mine, t_send.at[i], t_recv.at[i], dev)
-                  for i, dev in enumerate((partner, across, diag))]
-    for copy in tab_copies:
-        copy.start()
+
+    def kv_cross(count):
+        return remote(kv.at[pl.ds(0, count), :], kv.at[pl.ds(own, count), :], kv_sem.at[0], kv_sem.at[1], across)
+
+    def kv_send():
+        @pl.when(chip == 0)
+        def _():
+            kv_cross(own).start()
+
+        @pl.when(chip == 1)
+        def _():
+            kv_cross(red).start()
+
+
+    def build_picks():
+        with jax.named_scope('tab'):
+            for copy in tab_copies:
+                copy.wait()
+        lanes = tabs.shape[2]
+        tokens = pick_ref.shape[1]
+        held = pick_ref.shape[0] // tokens
+        before = lax.broadcasted_iota(jnp.int32, (lanes, lanes), 0) < lax.broadcasted_iota(jnp.int32, (lanes, lanes), 1)
+        before = jnp.where(before, 1.0, 0.0).astype(BF16)
+        dests, gates = [], []
+        for j in range(2):
+            dest, g = 0.0, 0.0
+            for i in range(2):
+                s = (chip if j == 0 else 1 - chip) * 2 + i
+                hits = tabs[s, experts:2 * experts, :]
+                rank = jnp.dot(hits.astype(BF16), before, preferred_element_type=F32)
+                at = jnp.where(hits > 0.5, rank + (s * tok + 1).astype(F32), 0.0)
+                gs = tabs[s, 0:experts, :]
+                dest = dest + (at if i == 0 else pltpu.roll(at, tok, 1))
+                g = g + (gs if i == 0 else pltpu.roll(gs, tok, 1))
+            dests.append(dest)
+            gates.append(g)
+        line = lax.broadcasted_iota(jnp.int32, (experts, lanes), 0)
+        slot = lax.broadcasted_iota(jnp.int32, (tokens, lanes), 0).astype(F32) + 1.0
+        for e in range(held):
+            total = jnp.zeros((tokens, 1), F32)
+            for j in range(2):
+                here = line == sp * held + e
+                dest = jnp.sum(jnp.where(here, dests[j], 0.0), axis=0, keepdims=True)
+                g = jnp.sum(jnp.where(here, gates[j], 0.0), axis=0, keepdims=True)
+                chosen = slot == dest
+                pick_ref[e * tokens:(e + 1) * tokens, j * lanes:(j + 1) * lanes] = jnp.where(chosen, 1.0, 0.0).astype(BF16)
+                total = total + jnp.sum(jnp.where(chosen, g, 0.0), axis=1, keepdims=True)
+            gate_ref[e * tokens:(e + 1) * tokens, :] = jnp.broadcast_to(total, (tokens, lanes))
+
 
     @pl.when(core == 0)
     def _():
+        kv_send()
         for k in range(AHEAD):
             with jax.named_scope('wxc0'):
                 x_cross(k).wait_recv()
@@ -183,6 +233,14 @@
         def _():
             with jax.named_scope('wxr'):
                 x_relay(k).wait_recv()
+
+        @pl.when(jnp.logical_and(core == 1, k == KV_STEP))
+        def _():
+            kv_send()
+
+        @pl.when(k == PICK_STEP)
+        def _():
+            build_picks()
 
         n = n_kv + k
         slot = n % RING
@@ -201,33 +259,47 @@
             def _():
                 load_wo(i)
 
-    with jax.named_scope('wkvx'):
-        kv_cross.wait()
-
     def o_pair(g):
         return remote(ob.at[:, pl.ds(pl.multiple_of(g * gw, HEAD), gw)],
                       ob.at[:, pl.ds(pl.multiple_of(half + g * gw, HEAD), gw)],
                       o_send.at[g], o_recv.at[g], partner)
 
-    @pl.loop(0, groups)
-    def _(g):
-        kg = kv[:, pl.ds(pl.multiple_of(g * HEAD, HEAD), HEAD)]
-        vt = jnp.transpose(kv[:, pl.ds(pl.multiple_of(kvw + g * HEAD, HEAD), HEAD)])
-        cols = [pl.ds(pl.multiple_of(g * gw + m * HEAD, HEAD), HEAD) for m in range(q_per)]
-        q = jnp.concatenate([acc[0:own, c].astype(BF16) for c in cols]
-                            + [acc[own:rows, c].astype(BF16) for c in cols], axis=0)
-        seen = jnp.concatenate([mask[:, 0:own]] * q_per + [mask[:, own:2 * own]] * (q_per * red // own), axis=1)
-        s = lax.dot_general(kg, q, (((1,), (1,)), ((), ())), preferred_element_type=F32)
-        s = jnp.where(seen > 0.5, s, MASKED)
-        top = jnp.max(s, axis=0, keepdims=True)
+    def attend(r0, r1, g, first, last, tri):
+        n = r1 - r0
+        cols = [slice(g * gw + m * HEAD, g * gw + (m + 1) * HEAD) for m in range(q_per)]
+        q = jnp.concatenate([acc[r0:r1, c].astype(BF16) for c in cols], axis=0)
+        s = lax.dot_general(q, kv[first:last, g * HEAD:(g + 1) * HEAD], (((1,), (1,)), ((), ())),
+                            preferred_element_type=F32)
+        lo, hi = tri - first, tri - first + n
+        que = lax.broadcasted_iota(jnp.int32, (q_per * n, n), 0) % n
+        key = lax.broadcasted_iota(jnp.int32, (q_per * n, n), 1)
+        parts = [s[:, :lo]] * (lo > 0) + [jnp.where(key <= que, s[:, lo:hi], MASKED)] + [s[:, hi:]] * (hi < last - first)
+        s = jnp.concatenate(parts, axis=1)
+        top = jnp.max(s, axis=1, keepdims=True)
         e = jnp.exp2((s - top) * EXP_SCALE)
-        w = (e * (1.0 / jnp.sum(e, axis=0, keepdims=True))).astype(BF16)
-        o = jnp.transpose(jnp.dot(vt, w, preferred_element_type=F32)).astype(BF16)
+        w = (e * (1.0 / jnp.sum(e, axis=1, keepdims=True))).astype(BF16)
+        o = jnp.dot(w, kv[first:last, kvw + g * HEAD:kvw + (g + 1) * HEAD], preferred_element_type=F32).astype(BF16)
         for m, c in enumerate(cols):
-            ob[0:own, c] = o[m * own:(m + 1) * own, :]
-            ob[own:rows, c] = o[q_per * own + m * red:q_per * own + (m + 1) * red, :]
-        with jax.named_scope('os'):
-            o_pair(g).start()
+            ob[r0:r1, c] = o[m * n:(m + 1) * n, :]
+
+    def heads(own_keys, red_keys):
+        for g in range(groups):
+            attend(0, own, g, *own_keys, 0)
+            attend(own, rows, g, *red_keys, own)
+            with jax.named_scope('os'):
+                o_pair(g).start()
+
+    @pl.when(chip == 0)
+    def _():
+        with jax.named_scope('wkvx'):
+            kv_cross(red).wait_recv()
+        heads((0, own), (0, own + red))
+
+    @pl.when(chip == 1)
+    def _():
+        with jax.named_scope('wkvx'):
+            kv_cross(own).wait_recv()
+        heads((0, 2 * own), (own, own + red))
 
     def h_cols(side, n):
         return pl.ds(pl.multiple_of((core if side == 0 else 1 - core) * oh + n * NC, HEAD), NC)
@@ -262,40 +334,6 @@
     for n in range(EARLY):
         wait_wo(n)
         oacc[n] = jnp.dot(ob[:, 0:half], wob[n, 0:half, :], preferred_element_type=F32)
-
-    with jax.named_scope('tab'):
-        for copy in tab_copies:
-            copy.wait()
-    lanes = tabs.shape[2]
-    held = pick_ref.shape[0] // pick_ref.shape[1]
-    tokens = pick_ref.shape[1]
-    before = lax.broadcasted_iota(jnp.int32, (lanes, lanes), 0) < lax.broadcasted_iota(jnp.int32, (lanes, lanes), 1)
-    before = jnp.where(before, 1.0, 0.0).astype(BF16)
-    dests, gates = [], []
-    for j in range(2):
-        dest, g = 0.0, 0.0
-        for i in range(2):
-            s = (chip if j == 0 else 1 - chip) * 2 + i
-            hits = tabs[s, experts:2 * experts, :]
-            rank = jnp.dot(hits.astype(BF16), before, preferred_element_type=F32)
-            at = jnp.where(hits > 0.5, rank + (s * tok + 1).astype(F32), 0.0)
-            gs = tabs[s, 0:experts, :]
-            dest = dest + (at if i == 0 else pltpu.roll(at, tok, 1))
-            g = g + (gs if i == 0 else pltpu.roll(gs, tok, 1))
-        dests.append(dest)
-        gates.append(g)
-    line = lax.broadcasted_iota(jnp.int32, (experts, lanes), 0)
-    slot = lax.broadcasted_iota(jnp.int32, (tokens, lanes), 0).astype(F32) + 1.0
-    for e in range(held):
-        total = jnp.zeros((tokens, 1), F32)
-        for j in range(2):
-            here = line == sp * held + e
-            dest = jnp.sum(jnp.where(here, dests[j], 0.0), axis=0, keepdims=True)
-            g = jnp.sum(jnp.where(here, gates[j], 0.0), axis=0, keepdims=True)
-            chosen = slot == dest
-            pick_ref[e * tokens:(e + 1) * tokens, j * lanes:(j + 1) * lanes] = jnp.where(chosen, 1.0, 0.0).astype(BF16)
-            total = total + jnp.sum(jnp.where(chosen, g, 0.0), axis=1, keepdims=True)
-        gate_ref[e * tokens:(e + 1) * tokens, :] = jnp.broadcast_to(total, (tokens, lanes))
 
     with jax.named_scope('wo'):
         @pl.loop(0, groups)
@@ -311,10 +349,13 @@
         with jax.named_scope('wwo'):
             wait_wo(slot)
         finish(n, jnp.dot(ob[...], wob[slot], preferred_element_type=F32))
-        relay(n - 2)
-
-    relay(nn - 2)
-    relay(nn - 1)
+
+        @pl.when(n >= LAG)
+        def _():
+            relay(n - LAG)
+
+    for n in range(LAG):
+        relay(nn - LAG + n)
 
     @pl.when(core == 0)
     def _():
@@ -322,6 +363,14 @@
         def _(k):
             x_cross(k).wait_send()
             x_relay(k).wait_send()
+
+    @pl.when(chip == 0)
+    def _():
+        kv_cross(own).wait_send()
+
+    @pl.when(chip == 1)
+    def _():
+        kv_cross(red).wait_send()
 
     with jax.named_scope('end'):
         @pl.loop(0, nn)
@@ -331,18 +380,27 @@
             h_relay(n).wait()
 
 
-def dispatch_kernel(pick_ref, gate_ref, h_ref, hid_ref, buf_ref):
-    tok, wide = hid_ref.shape
+def dispatch_kernel(pick_ref, gate_ref, h_ref, hid_ref, buf_ref, out, sems):
+    tok, d = hid_ref.shape
     held, tokens = buf_ref.shape[0], buf_ref.shape[1]
     core = lax.axis_index('sp') % 2
-    c = pl.ds(pl.multiple_of(pl.program_id(0) * wide, wide), wide)
-    hid_ref[...] = h_ref[pl.ds(pl.multiple_of(core * tok, 16), tok), c]
-    for e in range(held):
-        r = slice(e * tokens, (e + 1) * tokens)
-        y = jnp.dot(pick_ref[r, :], h_ref[:, c], preferred_element_type=F32)
-        g = gate_ref[r, :]
-        for j in range(0, wide, HEAD):
-            buf_ref[e, :, j:j + HEAD] = (g * y[:, j:j + HEAD]).astype(BF16)
+    own_rows = pl.ds(pl.multiple_of(core * tok, 16), tok)
+    copies = [pltpu.make_async_copy(h_ref.at[own_rows, :], hid_ref, sems.at[0])]
+    copies[0].start()
+    for i in range(d // WIDE):
+        c = slice(i * WIDE, (i + 1) * WIDE)
+        y = jnp.dot(pick_ref[...], h_ref[:, c], preferred_element_type=F32)
+        for e in range(held):
+            r = slice(e * tokens, (e + 1) * tokens)
+            g = gate_ref[r, :]
+            for j in range(0, WIDE, HEAD):
+                out[e, :, i * WIDE + j:i * WIDE + j + HEAD] = (g * y[r, j:j + HEAD]).astype(BF16)
+        part = pl.ds(i * WIDE, WIDE)
+        copy = pltpu.make_async_copy(out.at[:, :, part], buf_ref.at[:, :, part], sems.at[1 + i])
+        copy.start()
+        copies.append(copy)
+    for copy in copies:
+        copy.wait()
 
 
 def solution(mesh):
@@ -377,7 +435,6 @@
                 pltpu.VMEM((tokens, 2 * kvw), BF16),
                 pltpu.VMEM((rows, 2 * half), BF16),
                 pltpu.VMEM((EARLY, rows, NC), F32),
-                pltpu.VMEM((tokens, tokens), F32),
                 pltpu.VMEM((2, tok), jnp.int32),
                 pltpu.VMEM((experts, tok), F32),
                 pltpu.VMEM((group, 2 * experts, 128), F32),
@@ -391,15 +448,13 @@
                 collective_id=0, has_side_effects=True, vmem_limit_bytes=BLOCK_VMEM),
             name='block',
         )(x, w_q, w_k, w_v, w_o, ids.T, probs.T)
-        wide = 1024
         return pl.pallas_call(
             dispatch_kernel,
-            grid=(d // wide,),
             out_shape=(jax.ShapeDtypeStruct((tok, d), BF16),
                        jax.ShapeDtypeStruct((held, tokens, d), BF16)),
             in_specs=[vmem_spec] * 3,
-            out_specs=(pl.BlockSpec((tok, wide), lambda i: (0, i)),
-                       pl.BlockSpec((held, tokens, wide), lambda i: (0, 0, i))),
+            out_specs=(any_spec,) * 2,
+            scratch_shapes=[pltpu.VMEM((held, tokens, d), BF16), dma((1 + d // WIDE,))],
             compiler_params=pltpu.CompilerParams(vmem_limit_bytes=16_000_000),
             name='dispatch',
         )(pick, gate, h)

time: 46.3 us -> 42.2 us (0.911)
  Pallas kernels: 45.6 us -> 41.5 us
    pallas_call x1, Pallas kernels: 40.8 us -> 38.4 us  [device_step(): pl.pallas_call(block_kernel, out_shape=(OUT_SPACE((tokens, d), BF16), OUT...]
    pallas_call x1, Pallas kernels: 4.72 us -> 3.05 us  [device_step(): pl.pallas_call(dispatch_kernel, out_shape=(jax.ShapeDtypeStruct((tok, d),...]
where the time goes in v3:
time: 42.2 us; the launch traced here: 42.1 us
  Pallas kernels  41.5 us (98%)
  between operations  0.64 us (2%)
    pallas_call x1, Pallas kernels, device_step(): pl.pallas_call(block_kernel, out_shape=(OUT_SPACE((tokens, d), BF16), OUT...  38.4 us
    pallas_call x1, Pallas kernels, device_step(): pl.pallas_call(dispatch_kernel, out_shape=(jax.ShapeDtypeStruct((tok, d),...  3.05 us

profile of v3, /device:TPU:0, one launch (start us, length us, event | category | flops | bytes accessed | tf_op | source)
XLA Modules:
  0.0 42.1 jit_solution(14603704279816169036)
XLA Ops:
  0.6 38.4 %block.1 = (bf16[256,6144]{1,0:T(8,128)(2,1)S(1)}, bf16[512,256]{1,0:T(8,128)(2,1)S(1)}, f32[512,128]{1,0:T(8,128)S(1)}) custom-call(bf16[64,6144]{1,0:T(8,128)(2,1)} %x_ref.1, bf16[6144,6144]{1,0:T(8,128)(2,1)} %wq_ref.1, bf16[6144,1024]{1,0:T(8,128)(2,1)} %wk_ref.1, bf16[6144,1024]{1,0:T(8,128)(2,1)} %wv_ref.1, bf16[6144,6144]{1,0:T(8,128)(2,1)} %wo_ref.1, ...), custom_call_target="tpu_custom_call" | custom-call | tf_op jit(solution)/shard_map/block/pallas_call | solution.py:422
  39.1 3.0 %dispatch.1 = (bf16[64,6144]{1,0:T(8,128)(2,1)}, bf16[2,256,6144]{2,1,0:T(8,128)(2,1)}) custom-call(bf16[512,256]{1,0:T(8,128)(2,1)S(1)} %get-tuple-element.5.pick_ref, f32[512,128]{1,0:T(8,128)S(1)} %get-tuple-element.6.gate_ref, bf16[256,6144]{1,0:T(8,128)(2,1)S(1)} %get-tuple-element.7.h_ref), custom_call_target="tpu_custom_call" | custom-call | tf_op jit(solution)/shard_map/dispatch/pallas_call | solution.py:451

commit v4 on v3

--- a/solution.py
+++ b/solution.py
@@ -15,11 +15,11 @@
 NC = 512
 RING = 3
 WO_BUFS = 4
-AHEAD = 2
+AHEAD = 1
 EARLY = 2
 LAG = 3
 KV_STEP = 3
-PICK_STEP = 1
+PICK_STEP = 3
 WIDE = 512
 BLOCK_VMEM = 59_000_000
 OUT_SPACE = pltpu.VMEM
@@ -31,8 +31,7 @@
                  h_ref, pick_ref, gate_ref,
                  xb, ring, wob, acc, kvacc, kv, ob, oacc, idsb, probsb, tabs,
                  ring_sem, wo_sem, loc_sem, xp_sem, xc_send, xc_recv, xr_send, xr_recv,
-                 kv_sem, o_send, o_recv, hp_send, hp_recv, hc_send, hc_recv, hr_send, hr_recv,
-                 t_send, t_recv):
+                 kv_sem, o_sem, hp_sem, hc_send, hc_recv, hr_sem, t_sem):
     tok, d = x_ref.shape
     own = 2 * tok
     rows = xb.shape[0]
@@ -87,19 +86,39 @@
     def wait_wo(slot):
         pltpu.make_async_copy(wo_ref.at[:, pl.ds(0, NC)], wob.at[slot], wo_sem.at[slot]).wait()
 
+    barrier = pltpu.get_barrier_semaphore()
+    for dev in (partner, across, diag):
+        pl.semaphore_signal(barrier, inc=1, device_id={'sp': dev}, device_id_type=MESH)
+
     own_rows = pl.ds(pl.multiple_of(core * tok, 16), tok)
     x_load = pltpu.make_async_copy(x_ref, xb.at[own_rows, :], loc_sem.at[0])
-    for k in range(nk):
-        c = pl.ds(k * KC, KC)
-        pltpu.make_async_copy(x_ref.at[:, c], xb.at[own_rows, c], loc_sem.at[0]).start()
     ids_load = pltpu.make_async_copy(ids_ref, idsb, loc_sem.at[1])
     probs_load = pltpu.make_async_copy(probs_ref, probsb, loc_sem.at[2])
+    x_load.start()
     ids_load.start()
     probs_load.start()
     load_kv(0)
-    barrier = pltpu.get_barrier_semaphore()
-    for dev in (partner, across, diag):
-        pl.semaphore_signal(barrier, inc=1, device_id={'sp': dev}, device_id_type=MESH)
+
+    with jax.named_scope('bar'):
+        pl.semaphore_wait(barrier, 3)
+
+    x_pair = remote(x_ref, xb.at[own_rows, :], xp_sem.at[0], xp_sem.at[1], partner)
+    x_pair.start()
+
+    def x_cross(k):
+        c = pl.ds(pl.multiple_of(k * KC, KC), KC)
+        return remote(x_ref.at[:, c], xb.at[pl.ds(own, red), c], xc_send, xc_recv.at[k], across)
+
+    def x_relay(k):
+        c = pl.ds(pl.multiple_of(k * KC, KC), KC)
+        part = xb.at[pl.ds(own, red), c]
+        return remote(part, part, xr_send, xr_recv.at[k], partner)
+
+    @pl.when(core == 0)
+    def _():
+        for k in range(nk):
+            x_cross(k).start()
+
     with jax.named_scope('xl'):
         x_load.wait()
     for n in range(1, RING):
@@ -107,20 +126,6 @@
             load_kv(n)
         else:
             load_q(n)
-    with jax.named_scope('bar'):
-        pl.semaphore_wait(barrier, 3)
-
-    x_pair = remote(xb.at[own_rows, :], xb.at[own_rows, :], xp_sem.at[0], xp_sem.at[1], partner)
-    x_pair.start()
-
-    def x_cross(k):
-        c = pl.ds(pl.multiple_of(k * KC, KC), KC)
-        return remote(xb.at[pl.ds(0, red), c], xb.at[pl.ds(own, red), c], xc_send.at[k], xc_recv.at[k], across)
-
-    def x_relay(k):
-        c = pl.ds(pl.multiple_of(k * KC, KC), KC)
-        part = xb.at[pl.ds(own, red), c]
-        return remote(part, part, xr_send.at[k], xr_recv.at[k], partner)
 
     ids_load.wait()
     probs_load.wait()
@@ -136,15 +141,10 @@
     tabs[sp, 0:experts, 0:tok] = jnp.where(hit, pr / (p0 + p1), 0.0)
     tabs[sp, experts:2 * experts, 0:tok] = jnp.where(hit, 1.0, 0.0)
     mine = tabs.at[sp]
-    tab_copies = [remote(mine, mine, t_send.at[i], t_recv.at[i], dev)
+    tab_copies = [remote(mine, mine, t_sem.at[0], t_sem.at[1], dev)
                   for i, dev in enumerate((partner, across, diag))]
     for copy in tab_copies:
         copy.start()
-
-    @pl.when(core == 0)
-    def _():
-        for k in range(nk):
-            x_cross(k).start()
 
     acc[...] = jnp.zeros_like(acc)
     kvacc[...] = jnp.zeros_like(kvacc)
@@ -179,8 +179,8 @@
 
     def build_picks():
         with jax.named_scope('tab'):
-            for copy in tab_copies:
-                copy.wait()
+            three = tabs.at[pl.ds(0, 3)]
+            remote(three, three, t_sem.at[0], t_sem.at[1], partner).wait()
         lanes = tabs.shape[2]
         tokens = pick_ref.shape[1]
         held = pick_ref.shape[0] // tokens
@@ -254,15 +254,14 @@
             load_q(n + RING)
 
         late = n + RING - n_loads
-        for i, at in enumerate((0, 1, 2, 2)):
+        for i, at in enumerate((1, 2, 2, 2)):
             @pl.when(late == at)
             def _():
                 load_wo(i)
 
-    def o_pair(g):
-        return remote(ob.at[:, pl.ds(pl.multiple_of(g * gw, HEAD), gw)],
-                      ob.at[:, pl.ds(pl.multiple_of(half + g * gw, HEAD), gw)],
-                      o_send.at[g], o_recv.at[g], partner)
+    def o_pair(first, count):
+        return remote(ob.at[:, pl.ds(first * gw, count * gw)], ob.at[:, pl.ds(half + first * gw, count * gw)],
+                      o_sem.at[0], o_sem.at[1], partner)
 
     def attend(r0, r1, g, first, last, tri):
         n = r1 - r0
@@ -286,8 +285,11 @@
         for g in range(groups):
             attend(0, own, g, *own_keys, 0)
             attend(own, rows, g, *red_keys, own)
-            with jax.named_scope('os'):
-                o_pair(g).start()
+            if g == groups - 2:
+                with jax.named_scope('os'):
+                    o_pair(0, groups - 1).start()
+        with jax.named_scope('os'):
+            o_pair(groups - 1, 1).start()
 
     @pl.when(chip == 0)
     def _():
@@ -306,15 +308,15 @@
 
     def h_pair(n):
         part = h_ref.at[pl.ds(0, rows), h_cols(0, n)]
-        return remote(part, part, hp_send.at[n], hp_recv.at[n], partner)
+        return remote(part, part, hp_sem.at[0], hp_sem.at[1], partner)
 
     def h_cross(n):
         return remote(h_ref.at[pl.ds(red, own - red), h_cols(0, n)], h_ref.at[pl.ds(rows, own - red), h_cols(0, n)],
-                      hc_send.at[n], hc_recv.at[n], across)
+                      hc_send, hc_recv.at[n], across)
 
     def h_relay(n):
         part = h_ref.at[pl.ds(rows, own - red), h_cols(0, n)]
-        return remote(part, part, hr_send.at[n], hr_recv.at[n], partner)
+        return remote(part, part, hr_sem.at[0], hr_sem.at[1], partner)
 
     def relay(n):
         with jax.named_scope('whc'):
@@ -336,9 +338,7 @@
         oacc[n] = jnp.dot(ob[:, 0:half], wob[n, 0:half, :], preferred_element_type=F32)
 
     with jax.named_scope('wo'):
-        @pl.loop(0, groups)
-        def _(g):
-            o_pair(g).wait()
+        o_pair(0, groups).wait()
 
     for n in range(EARLY):
         finish(n, oacc[n] + jnp.dot(ob[:, half:2 * half], wob[n, half:2 * half, :], preferred_element_type=F32))
@@ -359,10 +359,9 @@
 
     @pl.when(core == 0)
     def _():
-        @pl.loop(0, nk)
-        def _(k):
-            x_cross(k).wait_send()
-            x_relay(k).wait_send()
+        part = xb.at[pl.ds(own, red), :]
+        remote(x_ref, part, xc_send, xc_recv.at[0], across).wait_send()
+        remote(part, part, xr_send, xr_recv.at[0], partner).wait_send()
 
     @pl.when(chip == 0)
     def _():
@@ -373,11 +372,11 @@
         kv_cross(red).wait_send()
 
     with jax.named_scope('end'):
-        @pl.loop(0, nn)
-        def _(n):
-            h_cross(n).wait_send()
-            h_pair(n).wait()
-            h_relay(n).wait()
+        shared = h_ref.at[pl.ds(0, rows), pl.ds(0, oh)]
+        late = h_ref.at[pl.ds(rows, own - red), pl.ds(0, oh)]
+        remote(late, late, hc_send, hc_recv.at[0], across).wait_send()
+        remote(shared, shared, hp_sem.at[0], hp_sem.at[1], partner).wait()
+        remote(late, late, hr_sem.at[0], hr_sem.at[1], partner).wait()
 
 
 def dispatch_kernel(pick_ref, gate_ref, h_ref, hid_ref, buf_ref, out, sems):
@@ -439,10 +438,8 @@
                 pltpu.VMEM((experts, tok), F32),
                 pltpu.VMEM((group, 2 * experts, 128), F32),
                 dma((RING,)), dma((WO_BUFS,)), dma((3,)), dma((2,)),
-                dma((nk,)), dma((nk,)), dma((nk,)), dma((nk,)),
-                dma((2,)), dma((kvw // HEAD,)), dma((kvw // HEAD,)),
-                dma((nn,)), dma((nn,)), dma((nn,)), dma((nn,)), dma((nn,)), dma((nn,)),
-                dma((3,)), dma((3,)),
+                dma(()), dma((nk,)), dma(()), dma((nk,)),
+                dma((2,)), dma((2,)), dma((2,)), dma(()), dma((nn,)), dma((2,)), dma((2,)),
             ],
             compiler_params=pltpu.CompilerParams(
                 collective_id=0, has_side_effects=True, vmem_limit_bytes=BLOCK_VMEM),

time: 42.2 us -> 40.3 us (0.955)
  Pallas kernels: 41.5 us -> 39.6 us
    pallas_call x1, Pallas kernels: 38.4 us -> 36.5 us  [device_step(): pl.pallas_call(block_kernel, out_shape=(OUT_SPACE((tokens, d), BF16), OUT...]
where the time goes in v4:
time: 40.3 us; the launch traced here: 40.2 us
  Pallas kernels  39.6 us (98%)
  between operations  0.64 us (2%)
    pallas_call x1, Pallas kernels, device_step(): pl.pallas_call(block_kernel, out_shape=(OUT_SPACE((tokens, d), BF16), OUT...  36.5 us
    pallas_call x1, Pallas kernels, device_step(): pl.pallas_call(dispatch_kernel, out_shape=(jax.ShapeDtypeStruct((tok, d),...  3.05 us

profile of v4, /device:TPU:0, one launch (start us, length us, event | category | flops | bytes accessed | tf_op | source)
XLA Modules:
  0.0 40.2 jit_solution(10470478704986840917)
XLA Ops:
  0.6 36.5 %block.1 = (bf16[256,6144]{1,0:T(8,128)(2,1)S(1)}, bf16[512,256]{1,0:T(8,128)(2,1)S(1)}, f32[512,128]{1,0:T(8,128)S(1)}) custom-call(bf16[64,6144]{1,0:T(8,128)(2,1)} %x_ref.1, bf16[6144,6144]{1,0:T(8,128)(2,1)} %wq_ref.1, bf16[6144,1024]{1,0:T(8,128)(2,1)} %wk_ref.1, bf16[6144,1024]{1,0:T(8,128)(2,1)} %wv_ref.1, bf16[6144,6144]{1,0:T(8,128)(2,1)} %wo_ref.1, ...), custom_call_target="tpu_custom_call" | custom-call | tf_op jit(solution)/shard_map/block/pallas_call | solution.py:421
  37.2 3.0 %dispatch.1 = (bf16[64,6144]{1,0:T(8,128)(2,1)}, bf16[2,256,6144]{2,1,0:T(8,128)(2,1)}) custom-call(bf16[512,256]{1,0:T(8,128)(2,1)S(1)} %get-tuple-element.5.pick_ref, f32[512,128]{1,0:T(8,128)S(1)} %get-tuple-element.6.gate_ref, bf16[256,6144]{1,0:T(8,128)(2,1)S(1)} %get-tuple-element.7.h_ref), custom_call_target="tpu_custom_call" | custom-call | tf_op jit(solution)/shard_map/dispatch/pallas_call | solution.py:448

commit v5 on v4

v5 whole, which is shorter than its diff:
```python
import math
import jax
import jax.numpy as jnp
from jax import lax
from jax.experimental import pallas as pl
from jax.experimental.pallas import tpu as pltpu
from jax.sharding import PartitionSpec as P

MESH = pl.DeviceIdType.MESH
HEAD = 128
SCALE = 1.0 / math.sqrt(HEAD)
EXP_SCALE = math.log2(math.e) * SCALE
MASKED = -1e30 / SCALE
KC = 1024
NC = 512
RING = 3
WO_BUFS = 4
RED = (80, 64)
EARLY = 2
LAG = 4
FIRST = 2
KV_STEP = 3
WIDE = 512
BLOCK_VMEM = 59_000_000
OUT_SPACE = pltpu.VMEM
F32 = jnp.float32
BF16 = jnp.bfloat16


def block_kernel(x_ref, wq_ref, wk_ref, wv_ref, wo_ref, ids_ref, probs_ref,
                 h_ref, pick_ref, gate_ref,
                 xb, ring, wob, acc, kvacc, kv, ob, oacc, idsb, probsb, tabs,
                 ring_sem, wo_sem, loc_sem, xp_sem, xc_send, xc_recv, xr_send, xr_recv,
                 kv_sem, o_sem, hp_sem, hc_send, hc_recv, hr_sem, t_sem):
    tok, d = x_ref.shape
    own = 2 * tok
    half = wq_ref.shape[1] // 2
    kvw = wk_ref.shape[1] // 2
    nk = d // KC
    per = half // (2 * kvw)
    n_kv = nk // per
    n_loads = n_kv + nk
    oh = d // 2
    nn = oh // NC
    groups = kvw // HEAD
    q_per = half // kvw
    gw = q_per * HEAD
    slots = [(n_loads - RING + i) % RING for i in range(2)]
    units = [(n * NC, NC, n) for n in range(WO_BUFS)]
    units += [((WO_BUFS + i) * NC, NC, slots[i]) for i in range(nn - WO_BUFS)]
    nu = len(units)

    sp = lax.axis_index('sp')
    chip = sp // 2
    core = sp % 2
    partner = chip * 2 + (1 - core)
    across = (1 - chip) * 2 + core
    diag = (1 - chip) * 2 + (1 - core)

    def remote(src, dst, send, recv, dev):
        return pltpu.make_async_remote_copy(
            src_ref=src, dst_ref=dst, send_sem=send, recv_sem=recv,
            device_id={'sp': dev}, device_id_type=MESH)

    def load_kv(n):
        for j in range(per):
            r = pl.ds((n * per + j) * KC, KC)
            c = pl.ds(pl.multiple_of(core * kvw, HEAD), kvw)
            pltpu.make_async_copy(wk_ref.at[r, c], ring.at[n, :, pl.ds(2 * j * kvw, kvw)], ring_sem.at[n]).start()
            pltpu.make_async_copy(wv_ref.at[r, c], ring.at[n, :, pl.ds((2 * j + 1) * kvw, kvw)], ring_sem.at[n]).start()

    def load_q(n):
        slot = n % RING
        r = pl.ds(pl.multiple_of((n - n_kv) * KC, KC), KC)
        c = pl.ds(pl.multiple_of(core * half, HEAD), half)
        pltpu.make_async_copy(wq_ref.at[r, c], ring.at[slot], ring_sem.at[slot]).start()

    def wait_ring(slot):
        pltpu.make_async_copy(wq_ref.at[pl.ds(0, KC), pl.ds(0, half)], ring.at[slot], ring_sem.at[slot]).wait()

    def wo_part(u, j):
        width, slot = units[u][1:]
        return slot, pl.ds(j * width, width)

    def wo_sem_of(u):
        return wo_sem.at[u] if u < WO_BUFS else ring_sem.at[units[u][2]]

    def load_wo(u):
        first, width, slot = units[u]
        c = pl.ds(pl.multiple_of(core * oh + first, HEAD), width)
        step = half if u < WO_BUFS else KC
        for j in range(2 * half // step):
            side = core if j * step < half else 1 - core
            r = pl.ds(pl.multiple_of(side * half + j * step % half, HEAD), step)
            if u < WO_BUFS:
                dst = wob.at[slot, pl.ds(j * step, step), :]
            else:
                dst = ring.at[slot, :, wo_part(u, j)[1]]
            pltpu.make_async_copy(wo_ref.at[r, c], dst, wo_sem_of(u)).start()

    def wait_wo(u):
        width, slot = units[u][1:]
        if u < WO_BUFS:
            copy = pltpu.make_async_copy(wo_ref.at[:, pl.ds(0, NC)], wob.at[slot], wo_sem_of(u))
        else:
            n = half * width // NC
            copy = pltpu.make_async_copy(wq_ref.at[pl.ds(0, KC), pl.ds(0, n)], ring.at[slot, :, pl.ds(0, n)], wo_sem_of(u))
        with jax.named_scope('wwo'):
            copy.wait()

    def times_wo(rows, u):
        slot = units[u][2]
        if u < WO_BUFS:
            return jnp.dot(ob[0:rows, :], wob[slot], preferred_element_type=F32)
        w = jnp.concatenate([ring[slot, :, wo_part(u, j)[1]] for j in range(2 * half // KC)], axis=0)
        return jnp.dot(ob[0:rows, :], w, preferred_element_type=F32)

    barrier = pltpu.get_barrier_semaphore()
    for dev in (partner, across, diag):
        pl.semaphore_signal(barrier, inc=1, device_id={'sp': dev}, device_id_type=MESH)

    own_rows = pl.ds(pl.multiple_of(core * tok, 16), tok)
    x_load = pltpu.make_async_copy(x_ref, xb.at[own_rows, :], loc_sem.at[0])
    ids_load = pltpu.make_async_copy(ids_ref, idsb, loc_sem.at[1])
    probs_load = pltpu.make_async_copy(probs_ref, probsb, loc_sem.at[2])
    x_load.start()
    ids_load.start()
    probs_load.start()
    load_kv(0)

    with jax.named_scope('bar'):
        pl.semaphore_wait(barrier, 3)

    x_pair = remote(x_ref, xb.at[own_rows, :], xp_sem.at[0], xp_sem.at[1], partner)
    x_pair.start()

    def share(c, k):
        return min(RED[c], tok) if k == 0 else max(RED[c] - tok, 0)

    def x_cross(c, k, j):
        n = share(c, k)
        cols = pl.ds(pl.multiple_of(j * KC, KC), KC)
        return remote(x_ref.at[pl.ds(0, n), cols], xb.at[pl.ds(own + k * tok, n), cols], xc_send, xc_recv.at[j], across)

    def x_relay(c, k, j):
        cols = pl.ds(pl.multiple_of(j * KC, KC), KC)
        part = xb.at[pl.ds(own + k * tok, share(c, k)), cols]
        return remote(part, part, xr_send, xr_recv.at[j], partner)

    for c in range(2):
        for k in range(2):
            if share(1 - c, k):
                @pl.when(jnp.logical_and(chip == c, core == k))
                def _():
                    for j in range(nk if k == 0 else FIRST):
                        x_cross(1 - c, k, j).start()

    with jax.named_scope('xl'):
        x_load.wait()
    for n in range(1, RING):
        if n < n_kv:
            load_kv(n)
        else:
            load_q(n)

    ids_load.wait()
    probs_load.wait()
    experts = probsb.shape[0]
    line = lax.broadcasted_iota(jnp.int32, (experts, tok), 0)
    pr = probsb[...]
    hit0 = line == idsb[0:1, :]
    hit1 = line == idsb[1:2, :]
    p0 = jnp.sum(jnp.where(hit0, pr, 0.0), axis=0, keepdims=True)
    p1 = jnp.sum(jnp.where(hit1, pr, 0.0), axis=0, keepdims=True)
    hit = jnp.logical_or(hit0, hit1)
    tabs[sp] = jnp.zeros(tabs.shape[1:], F32)
    tabs[sp, 0:experts, 0:tok] = jnp.where(hit, pr / (p0 + p1), 0.0)
    tabs[sp, experts:2 * experts, 0:tok] = jnp.where(hit, 1.0, 0.0)
    mine = tabs.at[sp]
    for dev in (partner, across, diag):
        remote(mine, mine, t_sem.at[0], t_sem.at[1], dev).start()

    acc[...] = jnp.zeros_like(acc)
    kvacc[...] = jnp.zeros_like(kvacc)

    with jax.named_scope('wxp'):
        x_pair.wait()

    @pl.loop(0, n_kv)
    def _(n):
        with jax.named_scope('wkv'):
            wait_ring(n)
        for j in range(per):
            c = pl.ds(pl.multiple_of((n * per + j) * KC, KC), KC)
            kvacc[...] += jnp.dot(xb[0:own, c], ring[n, :, 2 * j * kvw:2 * (j + 1) * kvw],
                                  preferred_element_type=F32)
        load_q(n + RING)

    for c in range(2):
        if share(1 - c, 1):
            @pl.when(jnp.logical_and(chip == c, core == 1))
            def _():
                for j in range(FIRST, nk):
                    x_cross(1 - c, 1, j).start()

    kv[0:own, :] = kvacc[...].astype(BF16)

    def build_picks():
        with jax.named_scope('tab'):
            three = tabs.at[pl.ds(0, 3)]
            remote(three, three, t_sem.at[0], t_sem.at[1], partner).wait()
        lanes = tabs.shape[2]
        tokens = pick_ref.shape[1]
        held = pick_ref.shape[0] // tokens
        before = lax.broadcasted_iota(jnp.int32, (lanes, lanes), 0) < lax.broadcasted_iota(jnp.int32, (lanes, lanes), 1)
        before = jnp.where(before, 1.0, 0.0).astype(BF16)
        dests, gates = [], []
        for j in range(2):
            dest, g = 0.0, 0.0
            for i in range(2):
                s = (chip if j == 0 else 1 - chip) * 2 + i
                hits = tabs[s, experts:2 * experts, :]
                rank = jnp.dot(hits.astype(BF16), before, preferred_element_type=F32)
                at = jnp.where(hits > 0.5, rank + (s * tok + 1).astype(F32), 0.0)
                gs = tabs[s, 0:experts, :]
                dest = dest + (at if i == 0 else pltpu.roll(at, tok, 1))
                g = g + (gs if i == 0 else pltpu.roll(gs, tok, 1))
            dests.append(dest)
            gates.append(g)
        line = lax.broadcasted_iota(jnp.int32, (experts, lanes), 0)
        slot = lax.broadcasted_iota(jnp.int32, (tokens, lanes), 0).astype(F32) + 1.0
        for e in range(held):
            total = jnp.zeros((tokens, 1), F32)
            for j in range(2):
                here = line == sp * held + e
                dest = jnp.sum(jnp.where(here, dests[j], 0.0), axis=0, keepdims=True)
                g = jnp.sum(jnp.where(here, gates[j], 0.0), axis=0, keepdims=True)
                chosen = slot == dest
                pick_ref[e * tokens:(e + 1) * tokens, j * lanes:(j + 1) * lanes] = jnp.where(chosen, 1.0, 0.0).astype(BF16)
                total = total + jnp.sum(jnp.where(chosen, g, 0.0), axis=1, keepdims=True)
            gate_ref[e * tokens:(e + 1) * tokens, :] = jnp.broadcast_to(total, (tokens, lanes))

    def rest(here):
        red = RED[here]
        rows = own + red
        given = RED[1 - here]
        kv_out, kv_in = (own, red) if here == 0 else (given, own)

        def kv_cross(count):
            return remote(kv.at[pl.ds(0, count), :], kv.at[pl.ds(own, count), :], kv_sem.at[0], kv_sem.at[1], across)

        def pass_on(j):
            for k in range(2):
                if share(here, k):
                    @pl.when(core == k)
                    def _():
                        with jax.named_scope('wxc'):
                            x_cross(here, k, j).wait_recv()
                        x_relay(here, k, j).start()

        @pl.when(core == 0)
        def _():
            kv_cross(kv_out).start()

        pass_on(0)

        @pl.loop(0, nk)
        def _(j):
            @pl.when(j + 1 < nk)
            def _():
                pass_on(j + 1)

            for k in range(2):
                if share(here, k):
                    @pl.when(core == 1 - k)
                    def _():
                        with jax.named_scope('wxr'):
                            x_relay(here, k, j).wait_recv()

            @pl.when(jnp.logical_and(core == 1, j == KV_STEP))
            def _():
                kv_cross(kv_out).start()

            n = n_kv + j
            slot = n % RING
            with jax.named_scope('wq'):
                wait_ring(slot)

            for i in range(2):
                @pl.when(j == nk - 2 + i)
                def _():
                    load_wo(i)

            c = pl.ds(pl.multiple_of(j * KC, KC), KC)
            acc[0:rows, :] += jnp.dot(xb[0:rows, c], ring[slot], preferred_element_type=F32)

            @pl.when(n + RING < n_loads)
            def _():
                load_q(n + RING)

        def o_pair(i):
            first, count = ((0, groups - 1), (groups - 1, 1))[i]
            return remote(ob.at[pl.ds(0, rows), pl.ds(first * gw, count * gw)],
                          ob.at[pl.ds(0, rows), pl.ds(half + first * gw, count * gw)],
                          o_sem.at[2 * i], o_sem.at[2 * i + 1], partner)

        def attend(r0, r1, g, first, last, tri):
            n = r1 - r0
            cols = [slice(g * gw + m * HEAD, g * gw + (m + 1) * HEAD) for m in range(q_per)]
            q = jnp.concatenate([acc[r0:r1, c].astype(BF16) for c in cols], axis=0)
            s = lax.dot_general(q, kv[first:last, g * HEAD:(g + 1) * HEAD], (((1,), (1,)), ((), ())),
                                preferred_element_type=F32)
            lo, hi = tri - first, tri - first + n
            seen = lax.broadcasted_iota(jnp.int32, (n, n), 1) <= lax.broadcasted_iota(jnp.int32, (n, n), 0)
            seen = jnp.concatenate([jnp.where(seen, 1.0, 0.0)] * q_per, axis=0) > 0.5
            parts = [s[:, :lo]] * (lo > 0) + [jnp.where(seen, s[:, lo:hi], MASKED)] + [s[:, hi:]] * (hi < last - first)
            s = jnp.concatenate(parts, axis=1)
            top = jnp.max(s, axis=1, keepdims=True)
            e = jnp.exp2((s - top) * EXP_SCALE)
            w = (e * (1.0 / jnp.sum(e, axis=1, keepdims=True))).astype(BF16)
            o = jnp.dot(w, kv[first:last, kvw + g * HEAD:kvw + (g + 1) * HEAD], preferred_element_type=F32).astype(BF16)
            for m, c in enumerate(cols):
                ob[r0:r1, c] = o[m * n:(m + 1) * n, :]

        load_wo(2)
        with jax.named_scope('wkvx'):
            kv_cross(kv_in).wait_recv()
        for g in range(groups):
            attend(0, own, g, 0, own if here == 0 else 2 * own, 0)
            attend(own, rows, g, 0 if here == 0 else own, rows, own)
            if g == groups - 2:
                with jax.named_scope('os'):
                    o_pair(0).start()
        with jax.named_scope('os'):
            o_pair(1).start()

        def h_cols(u):
            return pl.ds(pl.multiple_of(core * oh + units[u][0], HEAD), units[u][1])

        def h_pair(u):
            part = h_ref.at[pl.ds(0, rows), h_cols(u)]
            return remote(part, part, hp_sem.at[0], hp_sem.at[1], partner)

        def h_send(u):
            return remote(h_ref.at[pl.ds(given, own - given), h_cols(u)],
                          h_ref.at[pl.ds(own + given, own - given), h_cols(u)], hc_send, hc_recv.at[u], across)

        def relay(u):
            part = h_ref.at[pl.ds(rows, own - red), h_cols(u)]
            with jax.named_scope('whc'):
                remote(part, part, hc_send, hc_recv.at[u], across).wait_recv()
            remote(part, part, hr_sem.at[0], hr_sem.at[1], partner).start()

        def finish(u, total):
            h_ref[0:rows, h_cols(u)] = (xb[0:rows, h_cols(u)].astype(F32) + total).astype(BF16)
            h_send(u).start()
            h_pair(u).start()

        load_wo(3)
        for u in range(EARLY):
            wait_wo(u)
            oacc[u, 0:rows, :] = jnp.dot(ob[0:rows, 0:half], wob[u, 0:half, :], preferred_element_type=F32)
        load_wo(nu - 2)
        with jax.named_scope('wo'):
            o_pair(0).wait()
            o_pair(1).wait()
        for u in range(EARLY):
            finish(u, oacc[u, 0:rows, :] + jnp.dot(ob[0:rows, half:2 * half], wob[u, half:2 * half, :],
                                                   preferred_element_type=F32))
            if u == 0:
                load_wo(nu - 1)

        for u in range(EARLY, nu):
            wait_wo(u)
            finish(u, times_wo(rows, u))
            if u >= LAG:
                relay(u - LAG)
        build_picks()
        for u in range(nu - LAG, nu):
            relay(u)

        for k in range(2):
            if share(1 - here, k):
                @pl.when(core == k)
                def _():
                    n = share(1 - here, k)
                    part = xb.at[pl.ds(own + k * tok, n), :]
                    remote(x_ref.at[pl.ds(0, n), :], part, xc_send, xc_recv.at[0], across).wait_send()
            if share(here, k):
                @pl.when(core == k)
                def _():
                    part = xb.at[pl.ds(own + k * tok, share(here, k)), :]
                    remote(part, part, xr_send, xr_recv.at[0], partner).wait_send()
        kv_cross(kv_out).wait_send()

        with jax.named_scope('end'):
            sent = h_ref.at[pl.ds(given, own - given), pl.ds(0, oh)]
            shared = h_ref.at[pl.ds(0, rows), pl.ds(0, oh)]
            late = h_ref.at[pl.ds(rows, own - red), pl.ds(0, oh)]
            remote(sent, sent, hc_send, hc_recv.at[0], across).wait_send()
            remote(shared, shared, hp_sem.at[0], hp_sem.at[1], partner).wait()
            remote(late, late, hr_sem.at[0], hr_sem.at[1], partner).wait()

    for c in range(2):
        pl.when(chip == c)(lambda: rest(c))


def dispatch_kernel(pick_ref, gate_ref, h_ref, hid_ref, buf_ref, out, sems):
    tok, d = hid_ref.shape
    held, tokens = buf_ref.shape[0], buf_ref.shape[1]
    core = lax.axis_index('sp') % 2
    own_rows = pl.ds(pl.multiple_of(core * tok, 16), tok)
    copies = [pltpu.make_async_copy(h_ref.at[own_rows, :], hid_ref, sems.at[0])]
    copies[0].start()
    for i in range(d // WIDE):
        c = slice(i * WIDE, (i + 1) * WIDE)
        y = jnp.dot(pick_ref[...], h_ref[:, c], preferred_element_type=F32)
        for e in range(held):
            r = slice(e * tokens, (e + 1) * tokens)
            g = gate_ref[r, :]
            for j in range(0, WIDE, HEAD):
                out[e, :, i * WIDE + j:i * WIDE + j + HEAD] = (g * y[r, j:j + HEAD]).astype(BF16)
        part = pl.ds(i * WIDE, WIDE)
        copy = pltpu.make_async_copy(out.at[:, :, part], buf_ref.at[:, :, part], sems.at[1 + i])
        copy.start()
        copies.append(copy)
    for copy in copies:
        copy.wait()


def solution(mesh):
    row_spec = P(('dp', 'sp'), None)
    buf_spec = P(('dp', 'sp'), None, None)
    group = mesh.shape['sp']

    def device_step(x, w_q, w_k, w_v, w_o, ids, probs):
        tok, d = x.shape
        half, kvw, oh = w_q.shape[1] // 2, w_k.shape[1] // 2, d // 2
        experts = probs.shape[1]
        held = experts // group
        own, tokens = 2 * tok, group * tok
        rows = own + max(RED)
        nk, nn = d // KC, oh // NC
        any_spec = pl.BlockSpec(memory_space=pl.ANY)
        vmem_spec = pl.BlockSpec(memory_space=pltpu.VMEM)
        dma = pltpu.SemaphoreType.DMA
        h, pick, gate = pl.pallas_call(
            block_kernel,
            out_shape=(OUT_SPACE((tokens, d), BF16),
                       OUT_SPACE((held * tokens, tokens), BF16),
                       OUT_SPACE((held * tokens, 128), F32)),
            in_specs=[any_spec] * 7,
            out_specs=(vmem_spec,) * 3,
            scratch_shapes=[
                pltpu.VMEM((rows, d), BF16),
                pltpu.VMEM((RING, KC, half), BF16),
                pltpu.VMEM((WO_BUFS, d, NC), BF16),
                pltpu.VMEM((rows, half), F32),
                pltpu.VMEM((own, 2 * kvw), F32),
                pltpu.VMEM((tokens, 2 * kvw), BF16),
                pltpu.VMEM((rows, 2 * half), BF16),
                pltpu.VMEM((EARLY, rows, NC), F32),
                pltpu.VMEM((2, tok), jnp.int32),
                pltpu.VMEM((experts, tok), F32),
                pltpu.VMEM((group, 2 * experts, 128), F32),
                dma((RING,)), dma((WO_BUFS,)), dma((3,)), dma((2,)),
                dma(()), dma((nk,)), dma(()), dma((nk,)),
                dma((2,)), dma((4,)), dma((2,)), dma(()), dma((nn,)), dma((2,)), dma((2,)),
            ],
            compiler_params=pltpu.CompilerParams(
                collective_id=0, has_side_effects=True, vmem_limit_bytes=BLOCK_VMEM),
            name='block',
        )(x, w_q, w_k, w_v, w_o, ids.T, probs.T)
        return pl.pallas_call(
            dispatch_kernel,
            out_shape=(jax.ShapeDtypeStruct((tok, d), BF16),
                       jax.ShapeDtypeStruct((held, tokens, d), BF16)),
            in_specs=[vmem_spec] * 3,
            out_specs=(any_spec,) * 2,
            scratch_shapes=[pltpu.VMEM((held, tokens, d), BF16), dma((1 + d // WIDE,))],
            compiler_params=pltpu.CompilerParams(vmem_limit_bytes=16_000_000),
            name='dispatch',
        )(pick, gate, h)

    return jax.shard_map(device_step, mesh=mesh,
                         in_specs=(row_spec, P(), P(), P(), P(), row_spec, row_spec),
                         out_specs=(row_spec, buf_spec), check_vma=False)
```

time: 40.3 us -> 39.8 us (0.988)
  Pallas kernels: 39.6 us -> 38.9 us
    pallas_call x1, Pallas kernels: 36.5 us -> 35.9 us  [device_step(): pl.pallas_call(block_kernel, out_shape=(OUT_SPACE((tokens, d), BF16), OUT...]
where the time goes in v5:
time: 39.8 us; the launch traced here: 39.7 us
  Pallas kernels  38.9 us (98%)
  between operations  0.8 us (2%)
    pallas_call x1, Pallas kernels, device_step(): pl.pallas_call(block_kernel, out_shape=(OUT_SPACE((tokens, d), BF16), OUT...  35.9 us
    pallas_call x1, Pallas kernels, device_step(): pl.pallas_call(dispatch_kernel, out_shape=(jax.ShapeDtypeStruct((tok, d),...  3.05 us

profile of v5, /device:TPU:0, one launch (start us, length us, event | category | flops | bytes accessed | tf_op | source)
XLA Modules:
  0.0 39.7 jit_solution(1977751901118002232)
XLA Ops:
  0.6 35.9 %block.1 = (bf16[256,6144]{1,0:T(8,128)(2,1)S(1)}, bf16[512,256]{1,0:T(8,128)(2,1)S(1)}, f32[512,128]{1,0:T(8,128)S(1)}) custom-call(bf16[64,6144]{1,0:T(8,128)(2,1)} %x_ref.1, bf16[6144,6144]{1,0:T(8,128)(2,1)} %wq_ref.1, bf16[6144,1024]{1,0:T(8,128)(2,1)} %wk_ref.1, bf16[6144,1024]{1,0:T(8,128)(2,1)} %wv_ref.1, bf16[6144,6144]{1,0:T(8,128)(2,1)} %wo_ref.1, ...), custom_call_target="tpu_custom_call" | custom-call | tf_op jit(solution)/shard_map/block/pallas_call | solution.py:447
  36.5 3.0 %dispatch.1 = (bf16[64,6144]{1,0:T(8,128)(2,1)}, bf16[2,256,6144]{2,1,0:T(8,128)(2,1)}) custom-call(bf16[512,256]{1,0:T(8,128)(2,1)S(1)} %get-tuple-element.5.pick_ref, f32[512,128]{1,0:T(8,128)S(1)} %get-tuple-element.6.gate_ref, bf16[256,6144]{1,0:T(8,128)(2,1)S(1)} %get-tuple-element.7.h_ref), custom_call_target="tpu_custom_call" | custom-call | tf_op jit(solution)/shard_map/dispatch/pallas_call | solution.py:474

commit v6 on v5

--- a/solution.py
+++ b/solution.py
@@ -30,7 +30,7 @@
 def block_kernel(x_ref, wq_ref, wk_ref, wv_ref, wo_ref, ids_ref, probs_ref,
                  h_ref, pick_ref, gate_ref,
                  xb, ring, wob, acc, kvacc, kv, ob, oacc, idsb, probsb, tabs,
-                 ring_sem, wo_sem, loc_sem, xp_sem, xc_send, xc_recv, xr_send, xr_recv,
+                 ring_sem, half_sem, wo_sem, loc_sem, xp_sem, xc_send, xc_recv, xr_send, xr_recv,
                  kv_sem, o_sem, hp_sem, hc_send, hc_recv, hr_sem, t_sem):
     tok, d = x_ref.shape
     own = 2 * tok
@@ -75,6 +75,17 @@
         c = pl.ds(pl.multiple_of(core * half, HEAD), half)
         pltpu.make_async_copy(wq_ref.at[r, c], ring.at[slot], ring_sem.at[slot]).start()
 
+    def load_q_last():
+        slot = (n_loads - 1) % RING
+        c = pl.ds(pl.multiple_of(core * half, HEAD), half)
+        for i in range(2):
+            r = pl.ds(d - KC + i * KC // 2, KC // 2)
+            pltpu.make_async_copy(wq_ref.at[r, c], ring.at[slot, pl.ds(i * KC // 2, KC // 2), :], half_sem.at[i]).start()
+
+    def wait_half(slot, i):
+        r = pl.ds(i * KC // 2, KC // 2)
+        pltpu.make_async_copy(wq_ref.at[r, pl.ds(0, half)], ring.at[slot, r, :], half_sem.at[i]).wait()
+
     def wait_ring(slot):
         pltpu.make_async_copy(wq_ref.at[pl.ds(0, KC), pl.ds(0, half)], ring.at[slot], ring_sem.at[slot]).wait()
 
@@ -84,6 +95,9 @@
 
     def wo_sem_of(u):
         return wo_sem.at[u] if u < WO_BUFS else ring_sem.at[units[u][2]]
+
+    def wo_copy_sem(u, j):
+        return half_sem.at[j * KC // half] if u == nu - 1 else wo_sem_of(u)
 
     def load_wo(u):
         first, width, slot = units[u]
@@ -96,7 +110,7 @@
                 dst = wob.at[slot, pl.ds(j * step, step), :]
             else:
                 dst = ring.at[slot, :, wo_part(u, j)[1]]
-            pltpu.make_async_copy(wo_ref.at[r, c], dst, wo_sem_of(u)).start()
+            pltpu.make_async_copy(wo_ref.at[r, c], dst, wo_copy_sem(u, j)).start()
 
     def wait_wo(u):
         width, slot = units[u][1:]
@@ -108,12 +122,13 @@
         with jax.named_scope('wwo'):
             copy.wait()
 
-    def times_wo(rows, u):
+    def times_wo(o, u, first=0, last=2 * half):
         slot = units[u][2]
         if u < WO_BUFS:
-            return jnp.dot(ob[0:rows, :], wob[slot], preferred_element_type=F32)
-        w = jnp.concatenate([ring[slot, :, wo_part(u, j)[1]] for j in range(2 * half // KC)], axis=0)
-        return jnp.dot(ob[0:rows, :], w, preferred_element_type=F32)
+            w = wob[slot, first:last, :]
+        else:
+            w = jnp.concatenate([ring[slot, :, wo_part(u, j)[1]] for j in range(first // KC, last // KC)], axis=0)
+        return jnp.dot(o, w, preferred_element_type=F32)
 
     barrier = pltpu.get_barrier_semaphore()
     for dev in (partner, across, diag):
@@ -137,10 +152,10 @@
     def share(c, k):
         return min(RED[c], tok) if k == 0 else max(RED[c] - tok, 0)
 
-    def x_cross(c, k, j):
+    def x_cross(c, k, j, early=False):
         n = share(c, k)
         cols = pl.ds(pl.multiple_of(j * KC, KC), KC)
-        return remote(x_ref.at[pl.ds(0, n), cols], xb.at[pl.ds(own + k * tok, n), cols], xc_send, xc_recv.at[j], across)
+        return remote(x_ref.at[pl.ds(0, n), cols] if early else xb.at[pl.ds(k * tok, n), cols], xb.at[pl.ds(own + k * tok, n), cols], xc_send, xc_recv.at[j], across)
 
     def x_relay(c, k, j):
         cols = pl.ds(pl.multiple_of(j * KC, KC), KC)
@@ -152,11 +167,16 @@
             if share(1 - c, k):
                 @pl.when(jnp.logical_and(chip == c, core == k))
                 def _():
-                    for j in range(nk if k == 0 else FIRST):
-                        x_cross(1 - c, k, j).start()
+                    for j in range(FIRST):
+                        x_cross(1 - c, k, j, early=True).start()
 
     with jax.named_scope('xl'):
         x_load.wait()
+    for c in range(2):
+        @pl.when(jnp.logical_and(chip == c, core == 0))
+        def _():
+            for j in range(FIRST, nk):
+                x_cross(1 - c, 0, j).start()
     for n in range(1, RING):
         if n < n_kv:
             load_kv(n)
@@ -264,12 +284,7 @@
 
         pass_on(0)
 
-        @pl.loop(0, nk)
-        def _(j):
-            @pl.when(j + 1 < nk)
-            def _():
-                pass_on(j + 1)
-
+        def take_relay(j):
             for k in range(2):
                 if share(here, k):
                     @pl.when(core == 1 - k)
@@ -277,6 +292,11 @@
                         with jax.named_scope('wxr'):
                             x_relay(here, k, j).wait_recv()
 
+        @pl.loop(0, nk - 1)
+        def _(j):
+            pass_on(j + 1)
+            take_relay(j)
+
             @pl.when(jnp.logical_and(core == 1, j == KV_STEP))
             def _():
                 kv_cross(kv_out).start()
@@ -286,17 +306,31 @@
             with jax.named_scope('wq'):
                 wait_ring(slot)
 
-            for i in range(2):
-                @pl.when(j == nk - 2 + i)
-                def _():
-                    load_wo(i)
+            @pl.when(j == nk - 2)
+            def _():
+                load_wo(0)
 
             c = pl.ds(pl.multiple_of(j * KC, KC), KC)
             acc[0:rows, :] += jnp.dot(xb[0:rows, c], ring[slot], preferred_element_type=F32)
 
-            @pl.when(n + RING < n_loads)
+            @pl.when(n + RING < n_loads - 1)
             def _():
                 load_q(n + RING)
+
+            @pl.when(n + RING == n_loads - 1)
+            def _():
+                load_q_last()
+
+        take_relay(nk - 1)
+        slot = (n_loads - 1) % RING
+        for i in range(2):
+            with jax.named_scope('wqh'):
+                wait_half(slot, i)
+            if i == 0:
+                load_wo(1)
+            r = slice(i * KC // 2, (i + 1) * KC // 2)
+            acc[0:rows, :] += jnp.dot(xb[0:rows, d - KC + r.start:d - KC + r.stop], ring[slot, r, :],
+                                      preferred_element_type=F32)
 
         def o_pair(i):
             first, count = ((0, groups - 1), (groups - 1, 1))[i]
@@ -351,8 +385,11 @@
                 remote(part, part, hc_send, hc_recv.at[u], across).wait_recv()
             remote(part, part, hr_sem.at[0], hr_sem.at[1], partner).start()
 
+        def put(first, last, u, total):
+            h_ref[first:last, h_cols(u)] = (xb[first:last, h_cols(u)].astype(F32) + total).astype(BF16)
+
         def finish(u, total):
-            h_ref[0:rows, h_cols(u)] = (xb[0:rows, h_cols(u)].astype(F32) + total).astype(BF16)
+            put(0, rows, u, total)
             h_send(u).start()
             h_pair(u).start()
 
@@ -371,8 +408,23 @@
                 load_wo(nu - 1)
 
         for u in range(EARLY, nu):
-            wait_wo(u)
-            finish(u, times_wo(rows, u))
+            if u < nu - 1:
+                wait_wo(u)
+                finish(u, times_wo(ob[0:rows, :], u))
+            else:
+                first, last = (0, rows) if here == 0 else (given, own)
+                wait_half(units[u][2], 0)
+                oacc[0, first:last, :] = times_wo(ob[first:last, 0:half], u, 0, half)
+                with jax.named_scope('wwh'):
+                    wait_half(units[u][2], 1)
+                put(first, last, u, oacc[0, first:last, :] + times_wo(ob[first:last, half:2 * half], u, half, 2 * half))
+                h_send(u).start()
+                if here == 1:
+                    o = jnp.concatenate([ob[0:given, :], ob[own:rows, :]], axis=0)
+                    total = times_wo(o, u)
+                    put(0, given, u, total[0:given])
+                    put(own, rows, u, total[given:])
+                h_pair(u).start()
             if u >= LAG:
                 relay(u - LAG)
         build_picks()
@@ -410,8 +462,8 @@
     held, tokens = buf_ref.shape[0], buf_ref.shape[1]
     core = lax.axis_index('sp') % 2
     own_rows = pl.ds(pl.multiple_of(core * tok, 16), tok)
-    copies = [pltpu.make_async_copy(h_ref.at[own_rows, :], hid_ref, sems.at[0])]
-    copies[0].start()
+    hidden = pltpu.make_async_copy(h_ref.at[own_rows, :], hid_ref, sems.at[0])
+    hidden.start()
     for i in range(d // WIDE):
         c = slice(i * WIDE, (i + 1) * WIDE)
         y = jnp.dot(pick_ref[...], h_ref[:, c], preferred_element_type=F32)
@@ -421,11 +473,9 @@
             for j in range(0, WIDE, HEAD):
                 out[e, :, i * WIDE + j:i * WIDE + j + HEAD] = (g * y[r, j:j + HEAD]).astype(BF16)
         part = pl.ds(i * WIDE, WIDE)
-        copy = pltpu.make_async_copy(out.at[:, :, part], buf_ref.at[:, :, part], sems.at[1 + i])
-        copy.start()
-        copies.append(copy)
-    for copy in copies:
-        copy.wait()
+        pltpu.make_async_copy(out.at[:, :, part], buf_ref.at[:, :, part], sems.at[1]).start()
+    hidden.wait()
+    pltpu.make_async_copy(out, buf_ref, sems.at[1]).wait()
 
 
 def solution(mesh):
@@ -463,7 +513,7 @@
                 pltpu.VMEM((2, tok), jnp.int32),
                 pltpu.VMEM((experts, tok), F32),
                 pltpu.VMEM((group, 2 * experts, 128), F32),
-                dma((RING,)), dma((WO_BUFS,)), dma((3,)), dma((2,)),
+                dma((RING,)), dma((2,)), dma((WO_BUFS,)), dma((3,)), dma((2,)),
                 dma(()), dma((nk,)), dma(()), dma((nk,)),
                 dma((2,)), dma((4,)), dma((2,)), dma(()), dma((nn,)), dma((2,)), dma((2,)),
             ],
@@ -477,7 +527,7 @@
                        jax.ShapeDtypeStruct((held, tokens, d), BF16)),
             in_specs=[vmem_spec] * 3,
             out_specs=(any_spec,) * 2,
-            scratch_shapes=[pltpu.VMEM((held, tokens, d), BF16), dma((1 + d // WIDE,))],
+            scratch_shapes=[pltpu.VMEM((held, tokens, d), BF16), dma((2,))],
             compiler_params=pltpu.CompilerParams(vmem_limit_bytes=16_000_000),
             name='dispatch',
         )(pick, gate, h)

time: 39.8 us -> 39.2 us (0.985)
  Pallas kernels: 38.9 us -> 38.3 us
    pallas_call x1, Pallas kernels: 35.9 us -> 35.4 us  [device_step(): pl.pallas_call(block_kernel, out_shape=(OUT_SPACE((tokens, d), BF16), OUT...]
where the time goes in v6:
time: 39.2 us; the launch traced here: 39.1 us
  Pallas kernels  38.3 us (98%)
  between operations  0.8 us (2%)
    pallas_call x1, Pallas kernels, device_step(): pl.pallas_call(block_kernel, out_shape=(OUT_SPACE((tokens, d), BF16), OUT...  35.4 us
    pallas_call x1, Pallas kernels, device_step(): pl.pallas_call(dispatch_kernel, out_shape=(jax.ShapeDtypeStruct((tok, d),...  2.95 us

profile of v6, /device:TPU:0, one launch (start us, length us, event | category | flops | bytes accessed | tf_op | source)
XLA Modules:
  0.0 39.1 jit_solution(2101868979646388267)
XLA Ops:
  0.6 35.4 %block.1 = (bf16[256,6144]{1,0:T(8,128)(2,1)S(1)}, bf16[512,256]{1,0:T(8,128)(2,1)S(1)}, f32[512,128]{1,0:T(8,128)S(1)}) custom-call(bf16[64,6144]{1,0:T(8,128)(2,1)} %x_ref.1, bf16[6144,6144]{1,0:T(8,128)(2,1)} %wq_ref.1, bf16[6144,1024]{1,0:T(8,128)(2,1)} %wk_ref.1, bf16[6144,1024]{1,0:T(8,128)(2,1)} %wv_ref.1, bf16[6144,6144]{1,0:T(8,128)(2,1)} %wo_ref.1, ...), custom_call_target="tpu_custom_call" | custom-call | tf_op jit(solution)/shard_map/block/pallas_call | solution.py:497
  36.0 3.0 %dispatch.1 = (bf16[64,6144]{1,0:T(8,128)(2,1)}, bf16[2,256,6144]{2,1,0:T(8,128)(2,1)}) custom-call(bf16[512,256]{1,0:T(8,128)(2,1)S(1)} %get-tuple-element.5.pick_ref, f32[512,128]{1,0:T(8,128)S(1)} %get-tuple-element.6.gate_ref, bf16[256,6144]{1,0:T(8,128)(2,1)S(1)} %get-tuple-element.7.h_ref), custom_call_target="tpu_custom_call" | custom-call | tf_op jit(solution)/shard_map/dispatch/pallas_call | solution.py:524

commit v7 on v6

--- a/solution.py
+++ b/solution.py
@@ -196,10 +196,6 @@
     tabs[sp] = jnp.zeros(tabs.shape[1:], F32)
     tabs[sp, 0:experts, 0:tok] = jnp.where(hit, pr / (p0 + p1), 0.0)
     tabs[sp, experts:2 * experts, 0:tok] = jnp.where(hit, 1.0, 0.0)
-    mine = tabs.at[sp]
-    for dev in (partner, across, diag):
-        remote(mine, mine, t_sem.at[0], t_sem.at[1], dev).start()
-
     acc[...] = jnp.zeros_like(acc)
     kvacc[...] = jnp.zeros_like(kvacc)
 
@@ -357,6 +353,9 @@
                 ob[r0:r1, c] = o[m * n:(m + 1) * n, :]
 
         load_wo(2)
+        mine = tabs.at[sp]
+        for dev in (partner, across, diag):
+            remote(mine, mine, t_sem.at[0], t_sem.at[1], dev).start()
         with jax.named_scope('wkvx'):
             kv_cross(kv_in).wait_recv()
         for g in range(groups):
@@ -368,8 +367,8 @@
         with jax.named_scope('os'):
             o_pair(1).start()
 
-        def h_cols(u):
-            return pl.ds(pl.multiple_of(core * oh + units[u][0], HEAD), units[u][1])
+        def h_cols(u, side=core):
+            return pl.ds(pl.multiple_of(side * oh + units[u][0], HEAD), units[u][1])
 
         def h_pair(u):
             part = h_ref.at[pl.ds(0, rows), h_cols(u)]
@@ -377,12 +376,12 @@
 
         def h_send(u):
             return remote(h_ref.at[pl.ds(given, own - given), h_cols(u)],
-                          h_ref.at[pl.ds(own + given, own - given), h_cols(u)], hc_send, hc_recv.at[u], across)
+                          h_ref.at[pl.ds(own + given, own - given), h_cols(u)], hc_send, hc_recv.at[u], diag)
 
         def relay(u):
-            part = h_ref.at[pl.ds(rows, own - red), h_cols(u)]
+            part = h_ref.at[pl.ds(rows, own - red), h_cols(u, 1 - core)]
             with jax.named_scope('whc'):
-                remote(part, part, hc_send, hc_recv.at[u], across).wait_recv()
+                remote(part, part, hc_send, hc_recv.at[u], diag).wait_recv()
             remote(part, part, hr_sem.at[0], hr_sem.at[1], partner).start()
 
         def put(first, last, u, total):
@@ -449,7 +448,7 @@
             sent = h_ref.at[pl.ds(given, own - given), pl.ds(0, oh)]
             shared = h_ref.at[pl.ds(0, rows), pl.ds(0, oh)]
             late = h_ref.at[pl.ds(rows, own - red), pl.ds(0, oh)]
-            remote(sent, sent, hc_send, hc_recv.at[0], across).wait_send()
+            remote(sent, sent, hc_send, hc_recv.at[0], diag).wait_send()
             remote(shared, shared, hp_sem.at[0], hp_sem.at[1], partner).wait()
             remote(late, late, hr_sem.at[0], hr_sem.at[1], partner).wait()
 

time: 39.2 us -> 38.9 us (level)
  no operation moved by 1% of the time
where the time goes in v7:
time: 38.9 us; the launch traced here: 38.8 us
  Pallas kernels  38 us (98%)
  between operations  0.8 us (2%)
    pallas_call x1, Pallas kernels, device_step(): pl.pallas_call(block_kernel, out_shape=(OUT_SPACE((tokens, d), BF16), OUT...  35 us
    pallas_call x1, Pallas kernels, device_step(): pl.pallas_call(dispatch_kernel, out_shape=(jax.ShapeDtypeStruct((tok, d),...  2.95 us

profile of v7, /device:TPU:0, one launch (start us, length us, event | category | flops | bytes accessed | tf_op | source)
XLA Modules:
  0.0 38.8 jit_solution(18118490284981238121)
XLA Ops:
  0.6 35.0 %block.1 = (bf16[256,6144]{1,0:T(8,128)(2,1)S(1)}, bf16[512,256]{1,0:T(8,128)(2,1)S(1)}, f32[512,128]{1,0:T(8,128)S(1)}) custom-call(bf16[64,6144]{1,0:T(8,128)(2,1)} %x_ref.1, bf16[6144,6144]{1,0:T(8,128)(2,1)} %wq_ref.1, bf16[6144,1024]{1,0:T(8,128)(2,1)} %wk_ref.1, bf16[6144,1024]{1,0:T(8,128)(2,1)} %wv_ref.1, bf16[6144,6144]{1,0:T(8,128)(2,1)} %wo_ref.1, ...), custom_call_target="tpu_custom_call" | custom-call | tf_op jit(solution)/shard_map/block/pallas_call | solution.py:496
  35.7 3.0 %dispatch.1 = (bf16[64,6144]{1,0:T(8,128)(2,1)}, bf16[2,256,6144]{2,1,0:T(8,128)(2,1)}) custom-call(bf16[512,256]{1,0:T(8,128)(2,1)S(1)} %get-tuple-element.5.pick_ref, f32[512,128]{1,0:T(8,128)S(1)} %get-tuple-element.6.gate_ref, bf16[256,6144]{1,0:T(8,128)(2,1)S(1)} %get-tuple-element.7.h_ref), custom_call_target="tpu_custom_call" | custom-call | tf_op jit(solution)/shard_map/dispatch/pallas_call | solution.py:523

commit v8 on v7

--- a/solution.py
+++ b/solution.py
@@ -30,8 +30,8 @@
 def block_kernel(x_ref, wq_ref, wk_ref, wv_ref, wo_ref, ids_ref, probs_ref,
                  h_ref, pick_ref, gate_ref,
                  xb, ring, wob, acc, kvacc, kv, ob, oacc, idsb, probsb, tabs,
-                 ring_sem, half_sem, wo_sem, loc_sem, xp_sem, xc_send, xc_recv, xr_send, xr_recv,
-                 kv_sem, o_sem, hp_sem, hc_send, hc_recv, hr_sem, t_sem):
+                 ring_sem, half_sem, wo_sem, xp_sem, xc_send, xc_recv, xr_send, xr_recv,
+                 kv_sem, o_sem, hp_sem, hc_send, hc_recv, t_sem):
     tok, d = x_ref.shape
     own = 2 * tok
     half = wq_ref.shape[1] // 2
@@ -135,9 +135,9 @@
         pl.semaphore_signal(barrier, inc=1, device_id={'sp': dev}, device_id_type=MESH)
 
     own_rows = pl.ds(pl.multiple_of(core * tok, 16), tok)
-    x_load = pltpu.make_async_copy(x_ref, xb.at[own_rows, :], loc_sem.at[0])
-    ids_load = pltpu.make_async_copy(ids_ref, idsb, loc_sem.at[1])
-    probs_load = pltpu.make_async_copy(probs_ref, probsb, loc_sem.at[2])
+    x_load = pltpu.make_async_copy(x_ref, xb.at[own_rows, :], wo_sem.at[0])
+    ids_load = pltpu.make_async_copy(ids_ref, idsb, half_sem.at[0])
+    probs_load = pltpu.make_async_copy(probs_ref, probsb, half_sem.at[1])
     x_load.start()
     ids_load.start()
     probs_load.start()
@@ -382,7 +382,7 @@
             part = h_ref.at[pl.ds(rows, own - red), h_cols(u, 1 - core)]
             with jax.named_scope('whc'):
                 remote(part, part, hc_send, hc_recv.at[u], diag).wait_recv()
-            remote(part, part, hr_sem.at[0], hr_sem.at[1], partner).start()
+            remote(part, part, hp_sem.at[0], hp_sem.at[1], partner).start()
 
         def put(first, last, u, total):
             h_ref[first:last, h_cols(u)] = (xb[first:last, h_cols(u)].astype(F32) + total).astype(BF16)
@@ -446,11 +446,9 @@
 
         with jax.named_scope('end'):
             sent = h_ref.at[pl.ds(given, own - given), pl.ds(0, oh)]
-            shared = h_ref.at[pl.ds(0, rows), pl.ds(0, oh)]
-            late = h_ref.at[pl.ds(rows, own - red), pl.ds(0, oh)]
+            whole = h_ref.at[:, pl.ds(0, oh)]
             remote(sent, sent, hc_send, hc_recv.at[0], diag).wait_send()
-            remote(shared, shared, hp_sem.at[0], hp_sem.at[1], partner).wait()
-            remote(late, late, hr_sem.at[0], hr_sem.at[1], partner).wait()
+            remote(whole, whole, hp_sem.at[0], hp_sem.at[1], partner).wait()
 
     for c in range(2):
         pl.when(chip == c)(lambda: rest(c))
@@ -512,9 +510,9 @@
                 pltpu.VMEM((2, tok), jnp.int32),
                 pltpu.VMEM((experts, tok), F32),
                 pltpu.VMEM((group, 2 * experts, 128), F32),
-                dma((RING,)), dma((2,)), dma((WO_BUFS,)), dma((3,)), dma((2,)),
+                dma((RING,)), dma((2,)), dma((WO_BUFS,)), dma((2,)),
                 dma(()), dma((nk,)), dma(()), dma((nk,)),
-                dma((2,)), dma((4,)), dma((2,)), dma(()), dma((nn,)), dma((2,)), dma((2,)),
+                dma((2,)), dma((4,)), dma((2,)), dma(()), dma((nn,)), dma((2,)),
             ],
             compiler_params=pltpu.CompilerParams(
                 collective_id=0, has_side_effects=True, vmem_limit_bytes=BLOCK_VMEM),

time: 38.9 us -> 39.4 us (1.013)
  Pallas kernels: 38 us -> 38.5 us
    pallas_call x1, Pallas kernels: 35 us -> 35.6 us  [device_step(): pl.pallas_call(block_kernel, out_shape=(OUT_SPACE((tokens, d), BF16), OUT...]
where the time goes in v8:
time: 39.4 us; the launch traced here: 39.3 us
  Pallas kernels  38.5 us (98%)
  between operations  0.8 us (2%)
    pallas_call x1, Pallas kernels, device_step(): pl.pallas_call(block_kernel, out_shape=(OUT_SPACE((tokens, d), BF16), OUT...  35.6 us
    pallas_call x1, Pallas kernels, device_step(): pl.pallas_call(dispatch_kernel, out_shape=(jax.ShapeDtypeStruct((tok, d),...  2.95 us

profile of v8, /device:TPU:0, one launch (start us, length us, event | category | flops | bytes accessed | tf_op | source)
XLA Modules:
  0.0 39.3 jit_solution(6534961064515944626)
XLA Ops:
  0.6 35.6 %block.1 = (bf16[256,6144]{1,0:T(8,128)(2,1)S(1)}, bf16[512,256]{1,0:T(8,128)(2,1)S(1)}, f32[512,128]{1,0:T(8,128)S(1)}) custom-call(bf16[64,6144]{1,0:T(8,128)(2,1)} %x_ref.1, bf16[6144,6144]{1,0:T(8,128)(2,1)} %wq_ref.1, bf16[6144,1024]{1,0:T(8,128)(2,1)} %wk_ref.1, bf16[6144,1024]{1,0:T(8,128)(2,1)} %wv_ref.1, bf16[6144,6144]{1,0:T(8,128)(2,1)} %wo_ref.1, ...), custom_call_target="tpu_custom_call" | custom-call | tf_op jit(solution)/shard_map/block/pallas_call | solution.py:494
  36.2 3.0 %dispatch.1 = (bf16[64,6144]{1,0:T(8,128)(2,1)}, bf16[2,256,6144]{2,1,0:T(8,128)(2,1)}) custom-call(bf16[512,256]{1,0:T(8,128)(2,1)S(1)} %get-tuple-element.5.pick_ref, f32[512,128]{1,0:T(8,128)S(1)} %get-tuple-element.6.gate_ref, bf16[256,6144]{1,0:T(8,128)(2,1)S(1)} %get-tuple-element.7.h_ref), custom_call_target="tpu_custom_call" | custom-call | tf_op jit(solution)/shard_map/dispatch/pallas_call | solution.py:521
